TPU v7x, 32 devices: a whole 2x2x4 slice. The times are simulated.
32 devices in a mesh: dp: 16 (over z, x, core), ctx: 2 (over y).
Axes of the slice: x: 2, y: 2, z: 4, core: 2. Of those that a mesh axis runs over, the one named last changes fastest.
Arguments:
- tokens: bfloat16 [16, 1024, 768], P('dp', 'ctx'), may hold values from -6 to 6
- block_table: int32 [4], replicated, may hold values from 0 to 3, as said below
- ln1_gain: bfloat16 [768], P('dp'), may hold values from 0.099609375 to 1.8984375
- ln1_bias: bfloat16 [768], P('dp'), may hold values from -3 to 3
- w_qkv: bfloat16 [768, 2304], P('dp'), may hold values from -0.21875 to 0.21875
- bias_query: bfloat16 [768], P('dp'), may hold values from -3 to 3
- bias_value: bfloat16 [768], P('dp'), may hold values from -3 to 3
- w_out: bfloat16 [768, 768], P('dp'), may hold values from -6 to 6
- bias_out: bfloat16 [768], P('dp'), may hold values from -3 to 3
- ln2_gain: bfloat16 [768], P('dp'), may hold values from 0.099609375 to 1.8984375
- ln2_bias: bfloat16 [768], P('dp'), may hold values from -3 to 3
- w_up: bfloat16 [768, 3072], P('dp'), may hold values from -0.21875 to 0.21875
- bias_up: bfloat16 [3072], P('dp'), may hold values from -3 to 3
- w_down: bfloat16 [3072, 768], P('dp'), may hold values from -0.109375 to 0.109375
- bias_down: bfloat16 [768], P('dp'), may hold values from -3 to 3
- cotangent: bfloat16 [16, 1024, 768], P('dp', 'ctx'), may hold values from -6 to 6
Outputs:
- output: bfloat16 [16, 1024, 768], P('dp', 'ctx')
- grad_tokens: bfloat16 [16, 1024, 768], P('dp', 'ctx')
- grad_ln1_gain: float32 [768], P('dp')
- grad_ln1_bias: float32 [768], P('dp')
- grad_w_qkv: float32 [768, 2304], P('dp')
- grad_bias_query: float32 [768], P('dp')
- grad_bias_value: float32 [768], P('dp')
- grad_w_out: float32 [768, 768], P('dp')
- grad_bias_out: float32 [768], P('dp')
- grad_ln2_gain: float32 [768], P('dp')
- grad_ln2_bias: float32 [768], P('dp')
- grad_w_up: float32 [768, 3072], P('dp')
- grad_bias_up: float32 [3072], P('dp')
- grad_w_down: float32 [3072, 768], P('dp')
- grad_bias_down: float32 [768], P('dp')
Inputs may be any that keep to these rules, and one draw needn't show every extreme that they name: block_table holds every block index of a sequence once; entries 2 i and 2 i + 1 are a mirrored pair b and 3 - b.
All inputs are finite; a program needn't handle non-finite values.
Results may differ from a plain program's by a relative error of at most 0.018.
Values may be sent and summed in bfloat16 or wider, within the bound.
A program may use at most 256 MiB of HBM per device.

v0:
```python
import jax
import jax.numpy as jnp
from jax import lax
from jax.sharding import PartitionSpec as P

HEADS = 12
HD = 64
BLK = 256


def layer_norm(values, gain, shift):
    centred = values - jnp.mean(values, axis=-1, keepdims=True)
    spread_sq = jnp.mean(centred * centred, axis=-1, keepdims=True)
    return centred * lax.rsqrt(spread_sq + 1e-05) * gain + shift


def gelu_tanh(values):
    return jax.nn.gelu(values, approximate=True)


def pair_scores(queries, keyvals, allowed, pair_index, model_width):
    pair_width = 2 * HD
    query_part = lax.dynamic_slice_in_dim(queries, pair_index * pair_width, pair_width, 1).reshape(
        queries.shape[0], 2, HD
    )
    key_part = lax.dynamic_slice_in_dim(keyvals, pair_index * pair_width, pair_width, 1).reshape(
        keyvals.shape[0], 2, HD
    )
    value_part = lax.dynamic_slice_in_dim(
        keyvals, model_width + pair_index * pair_width, pair_width, 1
    ).reshape(keyvals.shape[0], 2, HD)
    scores = jnp.einsum(
        "thd,shd->hts", query_part, key_part, preferred_element_type=jnp.float32
    ) * HD ** (-0.5)
    scores = jnp.where(allowed[None], scores, -1e30)
    return (query_part, key_part, value_part, scores)


def shards(
    tokens,
    block_table,
    ln1_gain,
    ln1_bias,
    w_qkv,
    bias_query,
    bias_value,
    w_out,
    bias_out,
    ln2_gain,
    ln2_bias,
    w_up,
    bias_up,
    w_down,
    bias_down,
    cotangent,
):
    model_width = tokens.shape[2]
    row_count = tokens.shape[1]
    key_count = row_count * lax.axis_size("ctx")
    pair_width = 2 * HD
    scale = HD ** (-0.5)
    fetched = (
        lax.all_gather(ln1_gain, "dp", axis=0, tiled=True),
        lax.all_gather(ln1_bias, "dp", axis=0, tiled=True),
        lax.all_gather(w_qkv, "dp", axis=0, tiled=True),
        lax.all_gather(bias_query, "dp", axis=0, tiled=True),
        lax.all_gather(bias_value, "dp", axis=0, tiled=True),
        lax.all_gather(w_out, "dp", axis=0, tiled=True),
        lax.all_gather(bias_out, "dp", axis=0, tiled=True),
        lax.all_gather(ln2_gain, "dp", axis=0, tiled=True),
        lax.all_gather(ln2_bias, "dp", axis=0, tiled=True),
        lax.all_gather(w_up, "dp", axis=0, tiled=True),
        lax.all_gather(bias_up, "dp", axis=0, tiled=True),
        lax.all_gather(w_down, "dp", axis=0, tiled=True),
        lax.all_gather(bias_down, "dp", axis=0, tiled=True),
    )
    (
        gain_one,
        shift_one,
        qkv_w,
        query_b,
        value_b,
        out_w,
        out_b,
        gain_two,
        shift_two,
        up_w,
        up_b,
        down_w,
        down_b,
    ) = fetched
    inputs = tokens[0].astype(jnp.float32)
    normed_one, norm_one_back = jax.vjp(
        layer_norm, inputs, gain_one.astype(jnp.float32), shift_one.astype(jnp.float32)
    )
    normed_one_low = normed_one.astype(jnp.bfloat16)
    bias_cat = jnp.concatenate(
        [
            query_b.astype(jnp.float32),
            jnp.zeros((model_width,), jnp.float32),
            value_b.astype(jnp.float32),
        ]
    )
    projected = (
        jnp.dot(normed_one_low, qkv_w, preferred_element_type=jnp.float32) + bias_cat
    ).astype(jnp.bfloat16)
    queries = projected[:, :model_width]
    own_keyvals = projected[:, model_width:]
    keyvals = lax.all_gather(own_keyvals, "ctx", axis=0, tiled=True)
    per_device = row_count // BLK
    owned_blocks = lax.dynamic_slice_in_dim(
        block_table, lax.axis_index("ctx") * per_device, per_device
    )
    query_block = jnp.repeat(owned_blocks, BLK, total_repeat_length=row_count)
    key_block = jnp.repeat(block_table, BLK, total_repeat_length=key_count)
    allowed = key_block[None, :] <= query_block[:, None]

    def forward_pair(pair_index, state_pair):
        attended_acc, log_sums = state_pair
        query_part, key_part, value_part, scores = pair_scores(
            queries, keyvals, allowed, pair_index, model_width
        )
        largest = jnp.max(scores, axis=-1, keepdims=True)
        exponent = jnp.exp(scores - largest)
        row_total = jnp.sum(exponent, axis=-1, keepdims=True)
        probs_low = (exponent / row_total).astype(jnp.bfloat16)
        mixed_pair = jnp.einsum(
            "hts,shd->thd", probs_low, value_part, preferred_element_type=jnp.float32
        )
        attended_acc = lax.dynamic_update_slice_in_dim(
            attended_acc, mixed_pair.reshape(row_count, pair_width), pair_index * pair_width, 1
        )
        log_sums = lax.dynamic_update_slice_in_dim(
            log_sums, (largest + jnp.log(row_total))[..., 0], pair_index * 2, 0
        )
        return (attended_acc, log_sums)

    attended, log_sums = lax.fori_loop(
        0,
        HEADS // 2,
        forward_pair,
        (
            jnp.zeros((row_count, model_width), jnp.float32),
            jnp.zeros((HEADS, row_count), jnp.float32),
        ),
    )
    attended_low = attended.astype(jnp.bfloat16)
    branch = jnp.dot(attended_low, out_w, preferred_element_type=jnp.float32) + out_b.astype(
        jnp.float32
    )
    middle = inputs + branch
    normed_two, norm_two_back = jax.vjp(
        layer_norm, middle, gain_two.astype(jnp.float32), shift_two.astype(jnp.float32)
    )
    normed_two_low = normed_two.astype(jnp.bfloat16)
    hidden_pre = jnp.dot(normed_two_low, up_w, preferred_element_type=jnp.float32) + up_b.astype(
        jnp.float32
    )
    active, gelu_back = jax.vjp(gelu_tanh, hidden_pre)
    active_low = active.astype(jnp.bfloat16)
    result = middle + (
        jnp.dot(active_low, down_w, preferred_element_type=jnp.float32) + down_b.astype(jnp.float32)
    )
    output = result.astype(jnp.bfloat16)[None]
    again_weights = (
        lax.all_gather(w_qkv, "dp", axis=0, tiled=True),
        lax.all_gather(w_out, "dp", axis=0, tiled=True),
        lax.all_gather(w_up, "dp", axis=0, tiled=True),
        lax.all_gather(w_down, "dp", axis=0, tiled=True),
    )
    qkv_back_w, out_back_w, up_back_w, down_back_w = again_weights
    upstream = cotangent[0]
    grad_down_w = jnp.einsum("tf,td->fd", active_low, upstream, preferred_element_type=jnp.float32)
    grad_down_b = jnp.sum(upstream.astype(jnp.float32), axis=0)
    grad_active = jnp.einsum("td,fd->tf", upstream, down_back_w, preferred_element_type=jnp.float32)
    grad_hidden = gelu_back(grad_active)[0].astype(jnp.bfloat16)
    grad_up_w = jnp.einsum(
        "td,tf->df", normed_two_low, grad_hidden, preferred_element_type=jnp.float32
    )
    grad_up_b = jnp.sum(grad_hidden.astype(jnp.float32), axis=0)
    grad_normed_two = jnp.einsum(
        "tf,df->td", grad_hidden, up_back_w, preferred_element_type=jnp.float32
    )
    grad_middle_norm, grad_gain_two, grad_shift_two = norm_two_back(grad_normed_two)
    grad_middle = upstream.astype(jnp.float32) + grad_middle_norm
    grad_branch = grad_middle.astype(jnp.bfloat16)
    grad_out_w = jnp.einsum(
        "td,te->de", attended_low, grad_branch, preferred_element_type=jnp.float32
    )
    grad_out_b = jnp.sum(grad_branch.astype(jnp.float32), axis=0)
    grad_attended = jnp.einsum(
        "te,de->td", grad_branch, out_back_w, preferred_element_type=jnp.float32
    ).astype(jnp.bfloat16)

    def backward_pair(pair_index, state_pair):
        grad_queries, grad_keyvals = state_pair
        query_part, key_part, value_part, scores = pair_scores(
            queries, keyvals, allowed, pair_index, model_width
        )
        log_part = lax.dynamic_slice_in_dim(log_sums, pair_index * 2, 2, 0)[:, :, None]
        probs = jnp.exp(scores - log_part)
        grad_part = lax.dynamic_slice_in_dim(
            grad_attended, pair_index * pair_width, pair_width, 1
        ).reshape(row_count, 2, HD)
        grad_probs = jnp.einsum(
            "thd,shd->hts", grad_part, value_part, preferred_element_type=jnp.float32
        )
        inner_sum = jnp.sum(probs * grad_probs, axis=-1, keepdims=True)
        grad_scores = (probs * (grad_probs - inner_sum) * scale).astype(jnp.bfloat16)
        grad_query = jnp.einsum(
            "hts,shd->thd", grad_scores, key_part, preferred_element_type=jnp.float32
        )
        grad_key = jnp.einsum(
            "hts,thd->shd", grad_scores, query_part, preferred_element_type=jnp.float32
        )
        grad_value = jnp.einsum(
            "hts,thd->shd",
            probs.astype(jnp.bfloat16),
            grad_part,
            preferred_element_type=jnp.float32,
        )
        grad_queries = lax.dynamic_update_slice_in_dim(
            grad_queries, grad_query.reshape(row_count, pair_width), pair_index * pair_width, 1
        )
        grad_keyvals = lax.dynamic_update_slice_in_dim(
            grad_keyvals, grad_key.reshape(key_count, pair_width), pair_index * pair_width, 1
        )
        grad_keyvals = lax.dynamic_update_slice_in_dim(
            grad_keyvals,
            grad_value.reshape(key_count, pair_width),
            model_width + pair_index * pair_width,
            1,
        )
        return (grad_queries, grad_keyvals)

    grad_queries, grad_keyvals = lax.fori_loop(
        0,
        HEADS // 2,
        backward_pair,
        (
            jnp.zeros((row_count, model_width), jnp.float32),
            jnp.zeros((key_count, 2 * model_width), jnp.float32),
        ),
    )
    grad_keyvals_own = lax.psum_scatter(
        grad_keyvals.astype(jnp.bfloat16), "ctx", scatter_dimension=0, tiled=True
    ).astype(jnp.float32)
    grad_projected = jnp.concatenate([grad_queries, grad_keyvals_own], axis=1).astype(jnp.bfloat16)
    grad_qkv_w = jnp.einsum(
        "td,te->de", normed_one_low, grad_projected, preferred_element_type=jnp.float32
    )
    column_sums = jnp.sum(grad_projected.astype(jnp.float32), axis=0)
    grad_query_b = column_sums[:model_width]
    grad_value_b = column_sums[2 * model_width :]
    grad_normed_one = jnp.einsum(
        "te,de->td", grad_projected, qkv_back_w, preferred_element_type=jnp.float32
    )
    grad_inputs_norm, grad_gain_one, grad_shift_one = norm_one_back(grad_normed_one)
    grad_tokens = (grad_middle + grad_inputs_norm).astype(jnp.bfloat16)[None]
    summed_rows = (
        lax.psum_scatter(
            grad_gain_one.astype(jnp.bfloat16), "dp", scatter_dimension=0, tiled=True
        ).astype(jnp.float32),
        lax.psum_scatter(
            grad_shift_one.astype(jnp.bfloat16), "dp", scatter_dimension=0, tiled=True
        ).astype(jnp.float32),
        lax.psum_scatter(
            grad_qkv_w.astype(jnp.bfloat16), "dp", scatter_dimension=0, tiled=True
        ).astype(jnp.float32),
        lax.psum_scatter(
            grad_query_b.astype(jnp.bfloat16), "dp", scatter_dimension=0, tiled=True
        ).astype(jnp.float32),
        lax.psum_scatter(
            grad_value_b.astype(jnp.bfloat16), "dp", scatter_dimension=0, tiled=True
        ).astype(jnp.float32),
        lax.psum_scatter(
            grad_out_w.astype(jnp.bfloat16), "dp", scatter_dimension=0, tiled=True
        ).astype(jnp.float32),
        lax.psum_scatter(
            grad_out_b.astype(jnp.bfloat16), "dp", scatter_dimension=0, tiled=True
        ).astype(jnp.float32),
        lax.psum_scatter(
            grad_gain_two.astype(jnp.bfloat16), "dp", scatter_dimension=0, tiled=True
        ).astype(jnp.float32),
        lax.psum_scatter(
            grad_shift_two.astype(jnp.bfloat16), "dp", scatter_dimension=0, tiled=True
        ).astype(jnp.float32),
        lax.psum_scatter(
            grad_up_w.astype(jnp.bfloat16), "dp", scatter_dimension=0, tiled=True
        ).astype(jnp.float32),
        lax.psum_scatter(
            grad_up_b.astype(jnp.bfloat16), "dp", scatter_dimension=0, tiled=True
        ).astype(jnp.float32),
        lax.psum_scatter(
            grad_down_w.astype(jnp.bfloat16), "dp", scatter_dimension=0, tiled=True
        ).astype(jnp.float32),
        lax.psum_scatter(
            grad_down_b.astype(jnp.bfloat16), "dp", scatter_dimension=0, tiled=True
        ).astype(jnp.float32),
    )
    (
        sum_gain_one,
        sum_shift_one,
        sum_qkv_w,
        sum_query_b,
        sum_value_b,
        sum_out_w,
        sum_out_b,
        sum_gain_two,
        sum_shift_two,
        sum_up_w,
        sum_up_b,
        sum_down_w,
        sum_down_b,
    ) = summed_rows
    final_grads = (
        lax.psum(sum_gain_one.astype(jnp.bfloat16), "ctx").astype(jnp.float32),
        lax.psum(sum_shift_one.astype(jnp.bfloat16), "ctx").astype(jnp.float32),
        lax.psum(sum_qkv_w.astype(jnp.bfloat16), "ctx").astype(jnp.float32),
        lax.psum(sum_query_b.astype(jnp.bfloat16), "ctx").astype(jnp.float32),
        lax.psum(sum_value_b.astype(jnp.bfloat16), "ctx").astype(jnp.float32),
        lax.psum(sum_out_w.astype(jnp.bfloat16), "ctx").astype(jnp.float32),
        lax.psum(sum_out_b.astype(jnp.bfloat16), "ctx").astype(jnp.float32),
        lax.psum(sum_gain_two.astype(jnp.bfloat16), "ctx").astype(jnp.float32),
        lax.psum(sum_shift_two.astype(jnp.bfloat16), "ctx").astype(jnp.float32),
        lax.psum(sum_up_w.astype(jnp.bfloat16), "ctx").astype(jnp.float32),
        lax.psum(sum_up_b.astype(jnp.bfloat16), "ctx").astype(jnp.float32),
        lax.psum(sum_down_w.astype(jnp.bfloat16), "ctx").astype(jnp.float32),
        lax.psum(sum_down_b.astype(jnp.bfloat16), "ctx").astype(jnp.float32),
    )
    return (
        output,
        grad_tokens,
        final_grads[0],
        final_grads[1],
        final_grads[2],
        final_grads[3],
        final_grads[4],
        final_grads[5],
        final_grads[6],
        final_grads[7],
        final_grads[8],
        final_grads[9],
        final_grads[10],
        final_grads[11],
        final_grads[12],
    )


def solution(mesh):
    in_specs = (
        P("dp", "ctx", None),
        P(),
        P("dp"),
        P("dp"),
        P("dp", None),
        P("dp"),
        P("dp"),
        P("dp", None),
        P("dp"),
        P("dp"),
        P("dp"),
        P("dp", None),
        P("dp"),
        P("dp", None),
        P("dp"),
        P("dp", "ctx", None),
    )
    out_specs = (
        P("dp", "ctx", None),
        P("dp", "ctx", None),
        P("dp"),
        P("dp"),
        P("dp", None),
        P("dp"),
        P("dp"),
        P("dp", None),
        P("dp"),
        P("dp"),
        P("dp"),
        P("dp", None),
        P("dp"),
        P("dp", None),
        P("dp"),
    )
    return jax.shard_map(shards, mesh=mesh, in_specs=in_specs, out_specs=out_specs, check_vma=False)
```

profile of v0, /device:TPU:0, one launch (start us, length us, event | category | flops | bytes accessed | tf_op | source)
XLA Modules:
  0.0 855.8 jit_solution(569629735728347137)
XLA Ops:
  17.3 63.3 %all-reduce.19 = (bf16[768]{0:T(1024)(128)(2,1)S(1)}, bf16[768]{0:T(1024)(128)(2,1)S(1)}, bf16[768]{0:T(1024)(128)(2,1)S(1)}, bf16[768]{0:T(1024)(128)(2,1)S(1)}...) all-reduce(bf16[768]{0:T(1024)(128)(2,1)S(1)} %dynamic-update-slice, ...), channel_id=1, replica_groups=mesh['dp'=16,'ctx'=2] {'dp'}, use_global_device_ids=true, to_apply=%add.4 | all-reduce | flops 8448 | bytes 33792
  83.5 4.4 fusion.34
  97.4 34.4 %all-gather.8.cloned.1.call-done = bf16[1024,1536]{1,0:T(8,128)(2,1)} async-done(((bf16[512,1536]{1,0:T(8,128)(2,1)}), bf16[1024,1536]{1,0:T(8,128)(2,1)}) %all-gather.8.cloned.1.call-update) | async-done | bytes 3145744 | tf_op jit(solution)/shard_map/all_gather | solution.py:109
  131.8 4.7 copy.36
  136.6 57.0 %while.38 = (s32[]{:T(128)}, bf16[512,768]{0,1:T(8,128)(2,1)S(1)}, f32[12,512]{1,0:T(8,128)S(1)}, bf16[1024,1536]{0,1:T(8,128)(2,1)}, bf16[512,768]{0,1:T(8,128)...) while((s32[]{:T(128)}, bf16[512,768]{0,1:T(8,128)(2,1)S(1)}, ...), condition=%wide.region_5.6_spmd.clone, body=%wide.region_2.5_spmd.clone.sunk | while | flops 281541632 | bytes 33855824 | solution.py:138
  142.4 3.6 fusion.128
  151.9 3.6 fusion.128
  161.3 3.6 fusion.128
  170.8 3.6 fusion.128
  180.3 3.8 fusion.128
  189.9 3.6 fusion.128
  197.0 29.5 %all-gather.12.cloned.1.call-done = bf16[768,3072]{1,0:T(8,128)(2,1)} async-done(((bf16[48,3072]{1,0:T(8,128)(2,1)}), bf16[768,3072]{1,0:T(8,128)(2,1)}) %all-gather.12.cloned.1.call-update) | async-done | bytes 4718608 | tf_op jit(solution)/shard_map/all_gather | solution.py:72
  226.5 7.1 fusion.67
  233.6 46.7 %all-gather.14.cloned.1.call-done = bf16[3072,768]{1,0:T(8,128)(2,1)} async-done(((bf16[192,768]{1,0:T(8,128)(2,1)}), bf16[3072,768]{1,0:T(8,128)(2,1)}) %all-gather.14.cloned.1.call-update) | async-done | bytes 4718608 | tf_op jit(solution)/shard_map/all_gather | solution.py:74
  280.4 9.3 %fusion.77 = (bf16[3072]{0:T(1024)(128)(2,1)S(1)}, bf16[512,3072]{1,0:T(8,128)(2,1)S(1)}) fusion(f32[512,3072]{1,0:T(8,128)} %fusion.67, f32[3072]{0:T(1024)S(1)} %convert_element_type.214, bf16[3072,768]{1,0:T(8,128)(2,1)} %all-gather.14.cloned.1.call-done, bf16[1,512,768]{2,1,0:T(8,128)(2,1)S(1)} %copy-done.2), kind=kOutput, calls=%fused_computation.117 | convolution fusion | flops 2450519040 | bytes 14960640 | tf_op jit(solution)/shard_map/td,fd->tf/dot_general | solution.py:175
  289.7 3.0 multiply_reduce_fusion.1
  300.8 171.1 %while.39 = (s32[]{:T(128)}, bf16[512,768]{0,1:T(8,128)(2,1)}, bf16[1024,1536]{0,1:T(8,128)(2,1)}, bf16[1024,1536]{0,1:T(8,128)(2,1)}, bf16[512,768]{0,1:T(8,128...) while((s32[]{:T(128)}, bf16[512,768]{0,1:T(8,128)(2,1)}, ...), condition=%wide.region_12.13_spmd.clone, body=%wide.region_10.12_spmd.clone.sunk | while | flops 686297088 | bytes 35539284 | solution.py:236
  303.2 3.3 subtract_exponential_fusion.3
  310.2 7.1 fusion.141
  321.4 7.2 fusion.140
  331.7 3.3 subtract_exponential_fusion.3
  338.7 7.1 fusion.141
  350.0 7.2 fusion.140
  360.2 3.3 subtract_exponential_fusion.3
  367.3 7.1 fusion.141
  378.5 7.2 fusion.140
  388.8 3.3 subtract_exponential_fusion.3
  395.8 7.1 fusion.141
  407.0 7.2 fusion.140
  417.3 3.3 subtract_exponential_fusion.3
  424.3 7.1 fusion.141
  435.5 7.2 fusion.140
  445.8 3.3 subtract_exponential_fusion.3
  452.8 7.1 fusion.141
  464.0 7.2 fusion.140
  476.3 8.1 convolution_convert_fusion.1
  485.5 8.6 %convolution_convert_fusion = bf16[3072,768]{1,0:T(8,128)(2,1)} fusion(bf16[1,512,768]{2,1,0:T(8,128)(2,1)S(1)} %copy-done.3, f32[512,3072]{1,0:T(8,128)} %fusion.67, f32[3072]{0:T(1024)S(1)} %convert_element_type.214), kind=kOutput, calls=%fused_computation.50 | convolution fusion | flops 2434007040 | bytes 11808768 | tf_op jit(solution)/shard_map/tf,td->fd/dot_general | solution.py:173
  494.1 20.0 %reduce-scatter.6.cloned.1.call-done = bf16[512,1536]{0,1:T(8,128)(2,1)} async-done(((bf16[1024,1536]{0,1:T(8,128)(2,1)}), bf16[512,1536]{0,1:T(8,128)(2,1)}) %reduce-scatter.6.cloned.1.call-update) | async-done | bytes 1572880 | tf_op jit(solution)/shard_map/reduce_scatter | solution.py:245
  514.1 5.7 convolution_convert_fusion.2
  523.8 5.1 fusion.68
  531.0 61.1 %all-reduce.18 = (bf16[768]{0:T(1024)(128)(2,1)S(1)}, bf16[768]{0:T(1024)(128)(2,1)S(1)}, bf16[768]{0:T(1024)(128)(2,1)S(1)}, bf16[768]{0:T(1024)(128)(2,1)S(1)}...) all-reduce(bf16[768]{0:T(1024)(128)(2,1)S(1)} %dynamic-update-slice, ...), channel_id=1, replica_groups=mesh['dp'=16,'ctx'=2] {'dp'}, use_global_device_ids=true, to_apply=%add.8 | all-reduce | flops 9984 | bytes 39936
  592.7 5.0 all-reduce.20
  602.4 3.0 fusion.50
  605.4 49.0 %reduce-scatter.12.cloned.1.call-done = bf16[48,3072]{1,0:T(8,128)(2,1)} async-done(((bf16[768,3072]{1,0:T(8,128)(2,1)}), bf16[48,3072]{1,0:T(8,128)(2,1)}) %reduce-scatter.12.cloned.1.call-update) | async-done | bytes 294928 | tf_op jit(solution)/shard_map/reduce_scatter | solution.py:288
  654.4 78.7 %reduce-scatter.14.cloned.1.call-done = bf16[192,768]{1,0:T(8,128)(2,1)} async-done(((bf16[3072,768]{1,0:T(8,128)(2,1)}), bf16[192,768]{1,0:T(8,128)(2,1)}) %reduce-scatter.14.cloned.1.call-update) | async-done | bytes 294928 | tf_op jit(solution)/shard_map/reduce_scatter | solution.py:294
  733.1 71.1 %reduce-scatter.8.cloned.1.call-done = bf16[48,2304]{1,0:T(8,128)(2,1)} async-done(((bf16[768,2304]{1,0:T(8,128)(2,1)}), bf16[48,2304]{1,0:T(8,128)(2,1)}) %reduce-scatter.8.cloned.1.call-update) | async-done | bytes 221200 | tf_op jit(solution)/shard_map/reduce_scatter | solution.py:267
  804.2 9.5 %fusion.48 = bf16[1,512,768]{2,1,0:T(8,128)(2,1)} fusion(f32[512,768]{1,0:T(8,128)} %copy-done.4, bf16[3072,768]{1,0:T(8,128)(2,1)} %all-gather.14.cloned.1.call-done, f32[768]{0:T(1024)S(1)} %convert_element_type.216, f32[512,3072]{1,0:T(8,128)} %fusion.67, f32[3072]{0:T(1024)S(1)} %convert_element_type.214), kind=kOutput, calls=%fused_computation.82 | convolution fusion | flops 2432827392 | bytes 13384704 | tf_op jit(solution)/shard_map/dot_general | solution.py:162
  813.7 28.4 %all-reduce.24.cloned.1.call-done = (bf16[48,2304]{1,0:T(8,128)(2,1)}, bf16[48,768]{1,0:T(8,128)(2,1)}, bf16[48,3072]{1,0:T(8,128)(2,1)}, bf16[192,768]{1,0:T(8,128)(2,1)}) async-done(((bf16[48,2304]{1,0:T(8,128)(2,1)}, bf16[48,768]{1,0:T(8,128)(2,1)}, bf16[48,3072]{1,0:T(8,128)(2,1)}, bf16[192,768]{1,0:T(8,128)(2,1)}), (bf16[48,2304]{1,0:T(8,128)(2,1)}, bf16[48,768]{1,0:T(8,128)(2,1)}, ...) | async-done | bytes 884752 | tf_op jit(solution)/shard_map/psum | solution.py:319
  (265 shorter events, 154.9 us)
Async XLA Ops:
  7.2 76.3 %all-gather.6.cloned.1.call-start = ((), (), s32[]{:S(2)}) async-start(), calls=%async_computation.5 | async-start | bytes 3760128 | tf_op jit(solution)/shard_map/all_gather | solution.py:65
  7.9 123.8 %all-gather.8.cloned.1.call-start = ((), (), s32[]{:S(2)}) async-start(), calls=%async_computation.6 | async-start | bytes 4718592 | tf_op jit(solution)/shard_map/all_gather | solution.py:109
  87.9 3.9 copy-start.10
  87.9 5.1 copy-start.14
  88.0 6.4 copy-start.11
  88.0 6.4 copy-start.12
  88.0 6.4 copy-start.13
  89.3 104.3 %all-gather.10.cloned.1.call-start = ((), (), s32[]{:S(2)}) async-start(), calls=%async_computation.7 | async-start | bytes 1253376 | tf_op jit(solution)/shard_map/all_gather | solution.py:68
  90.0 136.5 %all-gather.12.cloned.1.call-start = ((), (), s32[]{:S(2)}) async-start(), calls=%async_computation.8 | async-start | bytes 5013504 | tf_op jit(solution)/shard_map/all_gather | solution.py:72
  90.6 189.7 %all-gather.14.cloned.1.call-start = ((), (), s32[]{:S(2)}) async-start(), calls=%async_computation.9 | async-start | bytes 5013504 | tf_op jit(solution)/shard_map/all_gather | solution.py:74
  91.2 422.9 %reduce-scatter.6.cloned.1.call-start = ((), (), s32[]{:S(2)}) async-start(), calls=%async_computation.10 | async-start | bytes 4718592 | tf_op jit(solution)/shard_map/reduce_scatter | solution.py:245
  136.6 57.9 %copy-start.1 = (bf16[1,512,768]{2,1,0:T(8,128)(2,1)S(1)}, bf16[1,512,768]{2,1,0:T(8,128)(2,1)}, u32[]{:S(2)}) copy-start(bf16[1,512,768]{2,1,0:T(8,128)(2,1)} %param.24) | copy-start | bytes 2359300
  139.2 2.0 copy-start
  148.7 2.0 copy-start
  158.1 2.0 copy-start
  167.6 2.0 copy-start
  177.1 2.0 copy-start
  186.7 2.0 copy-start
  193.6 0.9 copy-start.6
  193.6 3.4 copy-start.7
  196.7 93.0 %copy-start.4 = (f32[512,768]{1,0:T(8,128)}, f32[512,768]{1,0:T(8,128)S(1)}, u32[]{:S(2)}) copy-start(f32[512,768]{1,0:T(8,128)S(1)} %get-tuple-element.560) | copy-start | bytes 4718596
  197.0 83.3 %copy-start.2 = (bf16[1,512,768]{2,1,0:T(8,128)(2,1)S(1)}, bf16[1,512,768]{2,1,0:T(8,128)(2,1)}, u32[]{:S(2)}) copy-start(bf16[1,512,768]{2,1,0:T(8,128)(2,1)} %param.39) | copy-start | bytes 2359300
  280.3 9.4 %copy-start.15 = (bf16[768,3072]{1,0:T(8,128)(2,1)S(1)}, bf16[768,3072]{1,0:T(8,128)(2,1)}, u32[]{:S(2)}) copy-start(bf16[768,3072]{1,0:T(8,128)(2,1)} %all-gather.12.cloned.1.call-done) | copy-start | bytes 14155780
  289.7 3.0 copy-start.18
  292.7 3.3 copy-start.16
  295.2 0.9 copy-start.9
  471.9 1.1 copy-start.8
  471.9 133.4 %reduce-scatter.10.cloned.1.call-start = ((), (), s32[]{:S(2)}) async-start(), calls=%async_computation.12 | async-start | bytes 1253376 | tf_op jit(solution)/shard_map/reduce_scatter | solution.py:276
  476.0 178.4 %reduce-scatter.12.cloned.1.call-start = ((), (), s32[]{:S(2)}) async-start(), calls=%async_computation.13 | async-start | bytes 5013504 | tf_op jit(solution)/shard_map/reduce_scatter | solution.py:288
  484.3 1.1 copy-start.3
  484.4 248.7 %reduce-scatter.14.cloned.1.call-start = ((), (), s32[]{:S(2)}) async-start(), calls=%async_computation.14 | async-start | bytes 5013504 | tf_op jit(solution)/shard_map/reduce_scatter | solution.py:294
  494.1 310.1 %reduce-scatter.8.cloned.1.call-start = ((), (), s32[]{:S(2)}) async-start(), calls=%async_computation.11 | async-start | bytes 3760128 | tf_op jit(solution)/shard_map/reduce_scatter | solution.py:267
  519.8 1.8 copy-start.17
  519.8 322.4 %all-reduce.24.cloned.1.call-start = ((), (), s32[]{:S(2)}) async-start(), calls=%async_computation.15 | async-start | bytes 1769472 | tf_op jit(solution)/shard_map/psum | solution.py:319
  529.0 1.2 copy-start.5
Sparse Core Ops, SparseCore 0:
  10.3 50.2 all-gather.5
  89.4 42.2 all-gather.7
  134.0 38.2 all-gather.9
  174.5 51.9 all-gather.11
  228.6 51.6 all-gather.13
  472.1 41.9 reduce-scatter.5
  517.7 58.1 reduce-scatter.9
  579.7 74.6 reduce-scatter.11
  658.3 74.7 reduce-scatter.13
  736.8 67.3 reduce-scatter.7
  806.7 35.3 all-reduce.23
where the time goes:
time: 862 us; the launch traced here: 856 us
  waiting for transfers between devices  360 us (42%)
  matrix products  234 us (27%)
  blocking collectives  129 us (15%)
  local copies, waits for them, and re-layouts  74.3 us (9%)
  other arithmetic  38.5 us (4%)
  between operations  17.1 us (2%)
    unnamed x2, blocking collectives  124 us
    reduce_scatter x1, waiting for transfers between devices, shards(): lax.psum_scatter(grad_down_w.astype(jnp.bfloat16), 'dp', scatter_dimensio...  78.7 us
    reduce_scatter x1, waiting for transfers between devices, shards(): lax.psum_scatter(grad_qkv_w.astype(jnp.bfloat16), 'dp', scatter_dimension...  71.1 us
    reduce_scatter x1, waiting for transfers between devices, shards(): lax.psum_scatter(grad_up_w.astype(jnp.bfloat16), 'dp', scatter_dimension=...  49 us
    all_gather x1, waiting for transfers between devices, shards(): lax.all_gather(w_down, 'dp', axis=0, tiled=True)  46.7 us
    dot_general x6, matrix products, backward_pair(): jnp.einsum('hts,shd->thd', grad_scores, key_part, preferred_element_type=...  43.1 us
    dot_general x6, matrix products, backward_pair(): jnp.einsum('hts,thd->shd', grad_scores, query_part, preferred_element_typ...  42.6 us
    all_gather x1, waiting for transfers between devices, shards(): keyvals = lax.all_gather(own_keyvals, 'ctx', axis=0, tiled=True)  34.4 us
  transfers between devices with their start and end apart: 11, of which 8 were waited for; matrix products, arithmetic and copies ran while one was open for 15% of the time, Pallas kernels for 0%

commit v1 on v0

v1 whole, which is shorter than its diff:
```python
import functools
import jax
import jax.numpy as jnp
from jax import lax
from jax.experimental import pallas as pl
from jax.experimental.pallas import tpu as pltpu
from jax.sharding import PartitionSpec as P

ANY = pl.BlockSpec(memory_space=pl.ANY)
VM = pl.BlockSpec(memory_space=pltpu.VMEM)
DMA = pltpu.SemaphoreType.DMA


def near_first(count):
    order = []
    for step in range(1, count):
        order.append((step + 1) // 2 if step % 2 else count - step // 2)
    return order


class Spot:
    def __init__(self, dp, ctx):
        self.dp, self.ctx = dp, ctx
        self.lines = dp // 4
        me = lax.axis_index("dp")
        self.y = lax.axis_index("ctx")
        self.z = me // 4
        self.x = (me // 2) % 2
        self.c = me % 2
        self.me = me

    def dp_at(self, z, x, c):
        return (z * 2 + x) * 2 + c

    def z_at(self, k):
        return lax.rem(self.z + k, self.lines)

    def y_at(self, k):
        return lax.rem(self.y + k, self.ctx)

    def barrier(self):
        sem = pltpu.get_barrier_semaphore()
        peers = [{"dp": self.dp_at(self.z_at(k), self.x, self.c)} for k in range(1, self.lines)]
        peers.append({"dp": self.dp_at(self.z, 1 - self.x, self.c)})
        peers.append({"dp": self.dp_at(self.z, self.x, 1 - self.c)})
        peers += [{"ctx": self.y_at(k)} for k in range(1, self.ctx)]
        for peer in peers:
            pl.semaphore_signal(sem, inc=1, device_id=peer, device_id_type=pl.DeviceIdType.MESH)
        pl.semaphore_wait(sem, len(peers))


def remote(src, dst, ssem, rsem, device):
    return pltpu.make_async_remote_copy(
        src_ref=src, dst_ref=dst, send_sem=ssem, recv_sem=rsem,
        device_id=device, device_id_type=pl.DeviceIdType.MESH,
    )


def gather_kernel(dp, ctx, head, third, tok_ref, cat_ref, tok_all, wall,
                  loc, st, rt, sz, rz, sx, rx, sy, ry, sc, rc):
    at = Spot(dp, ctx)
    lines = at.lines
    ky = at.y % 2
    mine = pl.multiple_of(head + third + ky * third, 128)
    other = pl.multiple_of(head + third + (1 - ky) * third, 128)
    cols = {"q": pl.ds(0, head), "m": pl.ds(mine, third), "t": pl.ds(head, third), "o": pl.ds(other, third)}
    num = {"q": 0, "m": 1, "t": 2, "o": 3}
    own = at.me
    mate = {"dp": at.dp_at(at.z, at.x, 1 - at.c)}
    across = {"dp": at.dp_at(at.z, 1 - at.x, at.c)}
    pair = {"ctx": at.y + 1 - 2 * ky}
    at.barrier()
    copies = []

    def go(copy):
        copy.start()
        copies.append(copy)

    local = [pltpu.make_async_copy(cat_ref, wall.at[own], loc.at[0]),
             pltpu.make_async_copy(tok_ref, tok_all.at[at.y], loc.at[1])]
    for copy in local:
        copy.start()

    def block(b, z, x, c):
        return wall.at[at.dp_at(z, x, c), :, cols[b]]

    def own_block(b):
        return cat_ref.at[:, cols[b]]

    def send_z(b):
        for k in near_first(lines):
            go(remote(own_block(b), block(b, at.z, at.x, at.c), sz.at[num[b], k], rz.at[num[b], at.z],
                      {"dp": at.dp_at(at.z_at(k), at.x, at.c)}))

    def send_x(b, z, k, src):
        go(remote(src, block(b, z, at.x, at.c), sx.at[num[b], k], rx.at[num[b], z], across))

    def send_c(b, z, x, k, kx, src):
        go(remote(src, block(b, z, x, at.c), sc.at[num[b], k, kx], rc.at[num[b], z, x], mate))

    def send_y(z, x, k, kx, src):
        go(remote(src, block("m", z, x, at.c), sy.at[k, kx], ry.at[z, x], pair))

    def got_z(b, k):
        z = at.z_at(k)
        remote(own_block(b), block(b, z, at.x, at.c), sz.at[num[b], 0], rz.at[num[b], z], across).wait_recv()

    def got_x(b, k):
        z = at.z_at(k)
        remote(own_block(b), block(b, z, 1 - at.x, at.c), sz.at[num[b], 0], rx.at[num[b], z], across).wait_recv()

    def got_y(k, kx):
        z, x = at.z_at(k), (at.x + kx) % 2
        remote(own_block("o"), block("o", z, x, at.c), sz.at[0, 0], ry.at[z, x], across).wait_recv()

    def got_c(b, k, kx):
        z, x = at.z_at(k), (at.x + kx) % 2
        remote(own_block(b), block(b, z, x, 1 - at.c), sz.at[0, 0], rc.at[num[b], z, x], across).wait_recv()

    order = [0] + near_first(lines)
    for k in range(1, ctx):
        go(remote(tok_ref, tok_all.at[at.y], st.at[k], rt.at[at.y], {"ctx": at.y_at(k)}))
    for b in ("q", "m", "t"):
        send_z(b)
    for b in ("q", "m", "t"):
        send_x(b, at.z, 0, own_block(b))
        send_c(b, at.z, at.x, 0, 0, own_block(b))
        for k in order[1:]:
            got_z(b, k)
            z = at.z_at(k)
            src = block(b, z, at.x, at.c)
            send_x(b, z, k, src)
            if b == "m":
                send_y(z, at.x, k, 0, src)
            send_c(b, z, at.x, k, 0, src)
        for k in order:
            got_x(b, k)
            z = at.z_at(k)
            src = block(b, z, 1 - at.x, at.c)
            if b == "m":
                send_y(z, 1 - at.x, k, 1, src)
            send_c(b, z, 1 - at.x, k, 1, src)
    send_c("o", at.z, at.x, 0, 0, own_block("o"))
    for kx in range(2):
        for k in order:
            if k == 0 and kx == 0:
                continue
            got_y(k, kx)
            z, x = at.z_at(k), (at.x + kx) % 2
            send_c("o", z, x, k, kx, block("o", z, x, at.c))
    for b in ("q", "m", "t", "o"):
        for kx in range(2):
            for k in order:
                got_c(b, k, kx)
    for k in range(1, ctx):
        y = at.y_at(k)
        remote(tok_ref, tok_all.at[y], st.at[0], rt.at[y], across).wait_recv()
    for copy in copies:
        copy.wait_send()
    for copy in local:
        copy.wait()


def gather(tok, cat, dp, ctx, head, third):
    lines = dp // 4
    rows, width = cat.shape
    return pl.pallas_call(
        functools.partial(gather_kernel, dp, ctx, head, third),
        out_shape=(jax.ShapeDtypeStruct((ctx, *tok.shape), tok.dtype),
                   jax.ShapeDtypeStruct((dp, rows, width), cat.dtype)),
        in_specs=[VM, VM], out_specs=(ANY, ANY),
        scratch_shapes=[DMA((2,)), DMA((ctx,)), DMA((ctx,)),
                        DMA((3, lines)), DMA((3, lines)), DMA((3, lines)), DMA((3, lines)),
                        DMA((lines, 2)), DMA((lines, 2)), DMA((4, lines, 2)), DMA((4, lines, 2))],
        compiler_params=pltpu.CompilerParams(collective_id=0, has_side_effects=True, vmem_limit_bytes=32 * 2**20),
    )(tok, cat)


def scatter_kernel(dp, ctx, head, third, gq, gt, out, a_core, a_pair, a_x, a_z, a_y, stage, total,
                   loc, s1, r1, s2, r2, s3, r3, s4, r4, s5, r5):
    at = Spot(dp, ctx)
    lines = at.lines
    rows = gq.shape[1]
    ky = at.y % 2
    mine = pl.multiple_of(head + third + ky * third, 128)
    other = pl.multiple_of(head + third + (1 - ky) * third, 128)
    cols = {"q": pl.ds(0, head), "m": pl.ds(mine, third), "t": pl.ds(head, third), "o": pl.ds(other, third)}
    size = {"q": head, "m": third, "t": third, "o": third}
    num = {"q": 0, "m": 1, "t": 2, "o": 3}
    mate = {"dp": at.dp_at(at.z, at.x, 1 - at.c)}
    across = {"dp": at.dp_at(at.z, 1 - at.x, at.c)}
    pair = {"ctx": at.y + 1 - 2 * ky}
    at.barrier()
    copies = []

    def go(copy):
        copy.start()
        copies.append(copy)

    first = {"m": pl.multiple_of(third + ky * third, 128), "o": pl.multiple_of(third + (1 - ky) * third, 128), "t": 0}

    def full(b, at_dp):
        if b == "q":
            return gq.at[at_dp]
        return gt.at[at_dp, :, pl.ds(first[b], third)]

    order = [0] + near_first(lines)
    order = order[::-1]
    spots = [(k, kx) for kx in (1, 0) for k in order]

    def where(k, kx):
        return at.z_at(k), (at.x + kx) % 2

    def land(ref, b, *idx):
        return ref.at[(num[b], *idx, slice(None), pl.ds(0, size[b]))]

    blocks = ("o", "m", "t", "q")
    for b in blocks:
        for k, kx in spots:
            z, x = where(k, kx)
            go(remote(full(b, at.dp_at(z, x, 1 - at.c)), land(a_core, b, z, x),
                      s1.at[num[b], k, kx], r1.at[num[b], z, x], mate))
    def fetch(b, k, kx):
        z, x = where(k, kx)
        return pltpu.make_async_copy(full(b, at.dp_at(z, x, at.c)), land(stage, b, z, x),
                                     loc.at[num[b], k, kx])
    for b in blocks:
        for k, kx in spots:
            fetch(b, k, kx).start()

    def take(sem, dst):
        remote(dst, dst, s1.at[0, 0, 0], sem, across).wait_recv()

    def added(b, k, kx):
        z, x = where(k, kx)
        fetch(b, k, kx).wait()
        here = land(a_core, b, z, x)
        take(r1.at[num[b], z, x], here)
        here[...] = here[...] + land(stage, b, z, x)[...]
        return here

    for b in blocks:
        if b == "o":
            for k, kx in spots:
                z, x = where(k, kx)
                go(remote(added(b, k, kx), a_pair.at[z, x], s2.at[k, kx], r2.at[z, x], pair))
            continue
        for k, kx in spots:
            z, x = where(k, kx)
            here = added(b, k, kx)
            if b == "m":
                take(r2.at[z, x], a_pair.at[z, x])
                here[...] = here[...] + a_pair[z, x]
            if kx == 1:
                go(remote(here, land(a_x, b, z), s3.at[num[b], k], r3.at[num[b], z], across))
        for k in order:
            z = at.z_at(k)
            here = land(a_core, b, z, at.x)
            take(r3.at[num[b], z], land(a_x, b, z))
            here[...] = here[...] + land(a_x, b, z)[...]
            if k:
                go(remote(here, land(a_z, b, at.z), s4.at[num[b], k], r4.at[num[b], at.z],
                          {"dp": at.dp_at(z, at.x, at.c)}))
    for b in ("m", "t", "q"):
        acc = land(a_core, b, at.z, at.x)[...].astype(jnp.float32)
        for k in near_first(lines):
            z = at.z_at(k)
            take(r4.at[num[b], z], land(a_z, b, z))
            acc = acc + land(a_z, b, z)[...].astype(jnp.float32)
        land(total, b)[...] = acc
        land(a_core, b, at.z, at.x)[...] = acc.astype(jnp.bfloat16)
        for k in range(1, ctx):
            go(remote(land(a_core, b, at.z, at.x), land(a_y, b, at.y), s5.at[num[b], k], r5.at[num[b], at.y],
                      {"ctx": at.y_at(k)}))
    outs = []
    for b in ("t", "q", "m", "o"):
        if b == "m":
            acc = land(total, b)[...]
        elif b == "o":
            acc = jnp.zeros((rows, third), jnp.float32)
        else:
            acc = land(total, b)[...]
        for k in range(1, ctx):
            y = at.y_at(k)
            if b in ("t", "q") or (b == "m" and k % 2 == 0):
                take(r5.at[num[b], y], land(a_y, b, y))
                acc = acc + land(a_y, b, y)[...].astype(jnp.float32)
            elif b == "o" and k % 2 == 1:
                here = a_y.at[1, y, :, pl.ds(0, third)]
                take(r5.at[1, y], here)
                acc = acc + here[...].astype(jnp.float32)
        land(total, b)[...] = acc
        copy = pltpu.make_async_copy(land(total, b), out.at[:, cols[b]], loc.at[num[b], 0, 0])
        copy.start()
        outs.append(copy)
    for copy in copies:
        copy.wait_send()
    for copy in outs:
        copy.wait()


def scatter(gq, gt, dp, ctx, head, third):
    lines = dp // 4
    _, rows, width = gq.shape[0], gq.shape[1], gq.shape[2] + gt.shape[2]
    bf, f32 = jnp.bfloat16, jnp.float32
    return pl.pallas_call(
        functools.partial(scatter_kernel, dp, ctx, head, third),
        out_shape=jax.ShapeDtypeStruct((rows, width), f32),
        in_specs=[ANY, ANY], out_specs=ANY,
        scratch_shapes=[pltpu.VMEM((4, lines, 2, rows, head), bf), pltpu.VMEM((lines, 2, rows, third), bf),
                        pltpu.VMEM((3, lines, rows, head), bf), pltpu.VMEM((3, lines, rows, head), bf),
                        pltpu.VMEM((3, ctx, rows, head), bf), pltpu.VMEM((4, lines, 2, rows, head), bf),
                        pltpu.VMEM((4, rows, head), f32),
                        DMA((4, lines, 2)), DMA((4, lines, 2)), DMA((4, lines, 2)),
                        DMA((lines, 2)), DMA((lines, 2)),
                        DMA((3, lines)), DMA((3, lines)), DMA((3, lines)), DMA((3, lines)),
                        DMA((3, ctx)), DMA((3, ctx))],
        compiler_params=pltpu.CompilerParams(collective_id=1, has_side_effects=True, vmem_limit_bytes=60 * 2**20),
    )(gq, gt)


F32, BF = jnp.float32, jnp.bfloat16
HEADS, HD, BLK = 12, 64, 256
PAIRS, LANES = HEADS // 2, 2 * HD


def dot(a, b):
    return jnp.dot(a, b, preferred_element_type=F32)


def dot_t(a, b):
    return lax.dot_general(a, b, (((1,), (1,)), ((), ())), preferred_element_type=F32)


def dot_l(a, b):
    return lax.dot_general(a, b, (((0,), (0,)), ((), ())), preferred_element_type=F32)


def normed(x):
    centred = x - jnp.mean(x, axis=-1, keepdims=True)
    inv = lax.rsqrt(jnp.mean(centred * centred, axis=-1, keepdims=True) + 1e-05)
    return centred * inv, inv


def norm_back(dy, unit, inv, gain):
    dn = dy * gain
    return inv * (dn - jnp.mean(dn, axis=-1, keepdims=True) - unit * jnp.mean(dn * unit, axis=-1, keepdims=True))


class Table:
    def __init__(self, tbl, nb, y):
        self.nb, self.half = nb, nb // 2
        self.own = [tbl[2 * y], tbl[2 * y + 1]]
        first_high = (self.own[0] >= self.half).astype(jnp.int32)
        self.row_of = [first_high, 1 - first_high]
        self.slot_of = [first_high, 1 - first_high]
        self.block = [jnp.minimum(self.own[0], self.own[1]), jnp.maximum(self.own[0], self.own[1])]
        self.pos = []
        for j in range(nb):
            at = jnp.int32(0)
            for p in range(nb):
                at = at + jnp.where(tbl[p] == j, p, 0)
            self.pos.append(at)
        self.tbl = tbl

    def keys(self, slot):
        return self.half if slot == 0 else self.nb

    def masked(self, slot, j):
        return j >= 1 if slot == 0 else j > self.half


def rows_of(ref, *idx):
    value = ref[idx]
    return value.reshape(value.shape[0] * value.shape[1], value.shape[2])


def lane_masks(rows):
    lane = lax.broadcasted_iota(jnp.int32, (rows, LANES), 1)
    return [lane < HD, lane >= HD]


def project(ctx, tok, wall, h1, q, kv, vec, y):
    gain, shift = vec[0:1], vec[1:2]
    width = tok.shape[2]
    zero = jnp.zeros((1, width), F32)
    kv_bias = jnp.concatenate([zero, vec[3:4]], axis=1)
    w_kv = rows_of(wall, slice(None), slice(None), slice(128 + width, 128 + 3 * width))

    def rows(r, carry):
        x = tok[r // 2, pl.ds(pl.multiple_of((r % 2) * BLK, BLK), BLK)].astype(F32)
        low = (normed(x)[0] * gain + shift).astype(BF)
        kv[pl.ds(pl.multiple_of(r * BLK, BLK), BLK)] = (dot(low, w_kv) + kv_bias).astype(BF)
        return carry

    lax.fori_loop(0, 2 * ctx, rows, 0)
    w_q = rows_of(wall, slice(None), slice(None), slice(128, 128 + width))

    def own(i, carry):
        at = pl.ds(pl.multiple_of(i * BLK, BLK), BLK)
        low = (normed(tok[y, at].astype(F32))[0] * gain + shift).astype(BF)
        h1[at] = low
        q[at] = ((dot(low, w_q) + vec[2:3]).astype(BF).astype(F32) * HD ** (-0.5)).astype(BF)
        return carry

    lax.fori_loop(0, 2, own, 0)


def attend_pair(hp, table, q, kv, att, lse_acc, width):
    lanes = pl.ds(pl.multiple_of(hp * LANES, LANES), LANES)
    v_lanes = pl.ds(pl.multiple_of(width + hp * LANES, LANES), LANES)
    masks = lane_masks(BLK)
    lane = lax.broadcasted_iota(jnp.int32, (BLK, LANES), 1)
    for slot in range(2):
        q2 = q[pl.ds(pl.multiple_of(table.row_of[slot] * BLK, BLK), BLK), lanes]
        spots = [pl.ds(pl.multiple_of(table.pos[j] * BLK, BLK), BLK) for j in range(table.keys(slot))]
        mixed = []
        for h in range(2):
            qm = jnp.where(masks[h], q2, jnp.zeros_like(q2))
            scores = []
            for j, at in enumerate(spots):
                s = dot_t(qm, kv[at, lanes])
                if table.masked(slot, j):
                    s = jnp.where(j <= table.block[slot], s, -1e30)
                scores.append(s)
            largest = functools.reduce(jnp.maximum, scores)
            largest = jnp.max(largest, axis=-1, keepdims=True)
            exps = [jnp.exp(s - largest) for s in scores]
            total = jnp.sum(functools.reduce(jnp.add, exps), axis=-1, keepdims=True)
            out = functools.reduce(jnp.add, [dot(e.astype(BF), kv[at, v_lanes]) for e, at in zip(exps, spots)])
            mixed.append(out / total)
            lse_acc[slot] = jnp.where(lane == 2 * hp + h, largest + jnp.log(total), lse_acc[slot])
        att[slot, :, lanes] = jnp.where(masks[0], mixed[0], mixed[1]).astype(BF)


def attend_back_pair(hp, table, q, kv, da, lse, delta, dq, dk_acc, dv_acc, width):
    lanes = pl.ds(pl.multiple_of(hp * LANES, LANES), LANES)
    v_lanes = pl.ds(pl.multiple_of(width + hp * LANES, LANES), LANES)
    masks = lane_masks(BLK)
    for slot in (1, 0):
        row = pl.ds(pl.multiple_of(table.row_of[slot] * BLK, BLK), BLK)
        q2, da2 = q[row, lanes], da[row, lanes]
        dq_acc = None
        for h in range(2):
            qm = jnp.where(masks[h], q2, jnp.zeros_like(q2))
            dam = jnp.where(masks[h], da2, jnp.zeros_like(da2))
            lse_row = lse[slot, pl.ds(2 * hp + h, 1), :]
            delta_row = delta[table.row_of[slot], pl.ds(2 * hp + h, 1), :]
            for j in range(table.keys(slot)):
                at = pl.ds(pl.multiple_of(table.pos[j] * BLK, BLK), BLK)
                k2, v2 = kv[at, lanes], kv[at, v_lanes]
                st = dot_t(k2, qm)
                if table.masked(slot, j):
                    st = jnp.where(j <= table.block[slot], st, -1e30)
                pt = jnp.exp(st - lse_row)
                dst = (pt * (dot_t(v2, dam) - delta_row)).astype(BF)
                dv, dk = dot(pt.astype(BF), dam), dot(dst, qm)
                if slot == 1 and h == 0:
                    dv_acc[j], dk_acc[j] = dv, dk
                else:
                    dv_acc[j] += dv
                    dk_acc[j] += dk
                part = dot_l(dst, jnp.where(masks[h], k2, jnp.zeros_like(k2)))
                dq_acc = part if dq_acc is None else dq_acc + part
        dq[slot, :, lanes] = (dq_acc * HD ** (-0.5)).astype(BF)


def feed(nd, off_up, off_down, table, tok, att, wall, cot, vec, bup, out, gt, da, dx1, delta, gvec, gup,
         x1, h2, acc, dh2):
    rows, width = cot.shape
    dp, r = wall.shape[0], wall.shape[1]
    chunk = 4 * nd * r
    w_out = rows_of(wall, slice(None), slice(None), slice(off_up - width, off_up))
    for i in range(2):
        at = pl.ds(i * BLK, BLK)
        mid = tok[at].astype(F32) + (dot(att[table.slot_of[i]], w_out) + vec[4:5])
        x1[at] = mid
        h2[at] = (normed(mid)[0] * vec[5:6] + vec[6:7]).astype(BF)
        acc[at] = mid + vec[7:8]
    dh2[...] = jnp.zeros_like(dh2)
    g = cot[...]

    def part(f, carry):
        cols = pl.ds(pl.multiple_of(off_up + f * chunk, 128), chunk)
        w_up = rows_of(wall, slice(None), slice(None), cols)
        w_down = jnp.concatenate(
            [wall[f * nd + d, :, pl.ds(off_down + j * width, width)] for d in range(nd) for j in range(4)], axis=0)
        low = h2[...]
        u = dot(low, w_up) + bup[:, pl.ds(pl.multiple_of(f * chunk, 128), chunk)]
        sq = u * u
        t = jnp.tanh(u * (0.7978845608028654 + 0.03567740813636141 * sq))
        act = (0.5 * u * (1.0 + t)).astype(BF)
        slope = 0.5 * (1.0 + t) + 0.5 * u * (1.0 - t * t) * (0.7978845608028654 + 0.10703222440908423 * sq)
        acc[...] += dot(act, w_down)
        du = slope * dot_t(g, w_down)
        dul = du.astype(BF)
        gup[:, pl.ds(pl.multiple_of(f * chunk, 128), chunk)] = jnp.sum(dul.astype(F32), axis=0, keepdims=True)
        dh2[...] += dot_t(dul, w_up)
        g_up = dot_l(low, dul).astype(BF)
        gt[:, :, pl.ds(pl.multiple_of(width + f * chunk, 128), chunk)] = g_up.reshape(dp, r, chunk)
        g_down = dot_l(act, g).astype(BF)
        for d in range(nd):
            for j in range(4):
                piece = g_down[(4 * d + j) * r:(4 * d + j + 1) * r]
                gt[f * nd + d, :, pl.ds(width + off_down - off_up + j * width, width)] = piece
        return carry

    lax.fori_loop(0, dp // nd, part, 0)
    out[...] = acc[...].astype(BF)
    gf = g.astype(F32)
    unit, inv = normed(x1[...])
    dy = dh2[...]
    mid_grad = gf + norm_back(dy, unit, inv, vec[5:6])
    dx1[...] = mid_grad
    branch = mid_grad.astype(BF)
    gvec[...] = jnp.zeros_like(gvec)
    gvec[4:5] = jnp.sum(branch.astype(F32), axis=0, keepdims=True)
    gvec[5:6] = jnp.sum(dy * unit, axis=0, keepdims=True)
    gvec[6:7] = jnp.sum(dy, axis=0, keepdims=True)
    gvec[7:8] = jnp.sum(gf, axis=0, keepdims=True)
    head = lax.broadcasted_iota(jnp.int32, (16, width), 0)
    pick = (lax.broadcasted_iota(jnp.int32, (16, width), 1) // HD == head).astype(F32)
    grad = None
    for i in range(2):
        own = att[table.slot_of[i]]
        low = branch[i * BLK:(i + 1) * BLK]
        piece = dot_l(own, low)
        grad = piece if grad is None else grad + piece
        back = dot_t(low, w_out).astype(BF)
        da[pl.ds(i * BLK, BLK)] = back
        prod = back.astype(F32) * own.astype(F32)
        delta[i] = lax.dot_general(pick, prod, (((1,), (1,)), ((), ())), precision=lax.Precision.HIGHEST,
                                   preferred_element_type=F32)
    gt[:, :, 0:width] = grad.astype(BF).reshape(dp, r, width)


def last(ctx, table, y, dq, own_kv, h1, tok, wall, dx1, vec, gvec, gq, gtok):
    width = h1.shape[1]
    dp, r = wall.shape[0], wall.shape[1]
    w_q = rows_of(wall, slice(None), slice(None), slice(128, 128 + width))
    low = h1[...]
    dq_all = jnp.concatenate([dq[table.slot_of[0]], dq[table.slot_of[1]]], axis=0)
    gq[:, :, 128:128 + width] = dot_l(low, dq_all).astype(BF).reshape(dp, r, width)
    dh1 = dot_t(dq_all, w_q)
    dkv = own_kv()
    w_kv = rows_of(wall, slice(None), slice(None), slice(128 + width, 128 + 3 * width))
    gq[:, :, 128 + width:128 + 3 * width] = dot_l(low, dkv).astype(BF).reshape(dp, r, 2 * width)
    dh1 = dh1 + dot_t(dkv, w_kv)
    unit, inv = normed(tok[...].astype(F32))
    gtok[...] = (dx1[...] + norm_back(dh1, unit, inv, vec[0:1])).astype(BF)
    sums = [jnp.sum(dh1 * unit, axis=0, keepdims=True), jnp.sum(dh1, axis=0, keepdims=True),
            jnp.sum(dq_all.astype(F32), axis=0, keepdims=True),
            jnp.sum(dkv[:, width:].astype(F32), axis=0, keepdims=True)]
    table_rows = jnp.concatenate(sums + [gvec[4:16], jnp.zeros((112, width), F32)], axis=0)
    gq[:, :, 0:128] = jnp.transpose(table_rows).astype(BF).reshape(dp, r, 128)


SM = pl.BlockSpec(memory_space=pltpu.SMEM)


def params(limit, **more):
    return pltpu.CompilerParams(vmem_limit_bytes=limit * 2**20, **more)


def shape(*dims, dtype=BF):
    return jax.ShapeDtypeStruct(dims, dtype)


def attend_kernel(ctx, tbl, tok, wall, h1, q, kv, att, lse, vec, lse_acc):
    width = tok.shape[2]
    y = lax.axis_index("ctx")
    table = Table(tbl, 2 * ctx, y)
    small = rows_of(wall, slice(None), slice(None), slice(0, 128)).astype(F32)
    vec[...] = jnp.transpose(small)[0:16]
    project(ctx, tok, wall, h1, q, kv, vec, y)
    lse_acc[...] = jnp.zeros_like(lse_acc)

    def pair(hp, carry):
        attend_pair(hp, table, q, kv, att, lse_acc, width)
        return carry

    lax.fori_loop(0, PAIRS, pair, 0)
    for slot in range(2):
        lse[slot] = jnp.transpose(lse_acc[slot])[0:16]


def attend(tbl, tok_all, wall, ctx):
    rows, width = tok_all.shape[1:]
    return pl.pallas_call(
        functools.partial(attend_kernel, ctx),
        out_shape=(shape(rows, width), shape(rows, width), shape(ctx * rows, 2 * width), shape(2, BLK, width),
                   shape(2, 16, BLK, dtype=F32), shape(16, width, dtype=F32)),
        in_specs=[SM, VM, VM], out_specs=(VM,) * 6,
        scratch_shapes=[pltpu.VMEM((2, BLK, LANES), F32)],
        compiler_params=params(62), name="attend",
    )(tbl, tok_all, wall)


def feed_kernel(ctx, nd, off_up, off_down, tbl, tok, att, wall, cot, vec, bup, *rest):
    table = Table(tbl, 2 * ctx, lax.axis_index("ctx"))
    feed(nd, off_up, off_down, table, tok, att, wall, cot, vec, bup, *rest)


def feed_call(tbl, tok, att, wall, cot, vec, bup, ctx, off_up, off_down, gt_cols):
    rows, width = cot.shape
    dp, r = wall.shape[:2]
    return pl.pallas_call(
        functools.partial(feed_kernel, ctx, dp // 4, off_up, off_down),
        out_shape=(shape(rows, width), shape(dp, r, gt_cols), shape(rows, width), shape(rows, width, dtype=F32),
                   shape(2, 16, BLK, dtype=F32), shape(16, width, dtype=F32), shape(1, bup.shape[1], dtype=F32)),
        in_specs=[SM] + [VM] * 6, out_specs=(VM,) * 7,
        scratch_shapes=[pltpu.VMEM((rows, width), F32), pltpu.VMEM((rows, width), BF),
                        pltpu.VMEM((rows, width), F32), pltpu.VMEM((rows, width), F32)],
        compiler_params=params(62), name="feed",
    )(tbl, tok, att, wall, cot, vec, bup)


def attend_back_kernel(ctx, tbl, q, kv, da, lse, delta, dq, dkv, dk_acc, dv_acc):
    width = q.shape[1]
    table = Table(tbl, 2 * ctx, lax.axis_index("ctx"))

    def pair(hp, carry):
        attend_back_pair(hp, table, q, kv, da, lse, delta, dq, dk_acc, dv_acc, width)
        for j in range(2 * ctx):
            at = pl.ds(pl.multiple_of(table.pos[j] * BLK, BLK), BLK)
            dkv[at, pl.ds(pl.multiple_of(hp * LANES, LANES), LANES)] = dk_acc[j].astype(BF)
            dkv[at, pl.ds(pl.multiple_of(width + hp * LANES, LANES), LANES)] = dv_acc[j].astype(BF)
        return carry

    lax.fori_loop(0, PAIRS, pair, 0)


def attend_back(tbl, q, kv, da, lse, delta, ctx):
    rows, width = q.shape
    return pl.pallas_call(
        functools.partial(attend_back_kernel, ctx),
        out_shape=(shape(2, BLK, width), shape(*kv.shape)),
        in_specs=[SM] + [VM] * 5, out_specs=(VM,) * 2,
        scratch_shapes=[pltpu.VMEM((2 * ctx, BLK, LANES), F32), pltpu.VMEM((2 * ctx, BLK, LANES), F32)],
        compiler_params=params(62), name="attend_back",
    )(tbl, q, kv, da, lse, delta)


def last_kernel(ctx, tbl, dq, dkv, h1, tok, wall, dx1, vec, gvec, gq, gtok, land, ssem, rsem):
    rows = h1.shape[0]
    y = lax.axis_index("ctx")
    table = Table(tbl, 2 * ctx, y)
    sem = pltpu.get_barrier_semaphore()
    peers = [lax.rem(y + k, ctx) for k in range(1, ctx)]
    for peer in peers:
        pl.semaphore_signal(sem, inc=1, device_id={"ctx": peer}, device_id_type=pl.DeviceIdType.MESH)
    pl.semaphore_wait(sem, ctx - 1)
    copies = []
    for k, peer in enumerate(peers):
        copy = remote(dkv.at[pl.ds(pl.multiple_of(peer * rows, BLK), rows)], land.at[y], ssem.at[k], rsem.at[y], {"ctx": peer})
        copy.start()
        copies.append(copy)

    def own_kv():
        total = dkv[pl.ds(pl.multiple_of(y * rows, BLK), rows)].astype(F32)
        for peer in peers:
            remote(land.at[peer], land.at[peer], ssem.at[0], rsem.at[peer], {"ctx": peer}).wait_recv()
            total = total + land[peer].astype(F32)
        return total.astype(BF)

    last(ctx, table, y, dq, own_kv, h1, tok, wall, dx1, vec, gvec, gq, gtok)
    for copy in copies:
        copy.wait_send()


def last_call(tbl, dq, dkv, h1, tok, wall, dx1, vec, gvec, ctx, head):
    rows, width = h1.shape
    dp, r = wall.shape[:2]
    return pl.pallas_call(
        functools.partial(last_kernel, ctx),
        out_shape=(shape(dp, r, head), shape(rows, width)),
        in_specs=[SM] + [VM] * 8, out_specs=(VM,) * 2,
        scratch_shapes=[pltpu.VMEM((ctx, rows, 2 * width), BF), DMA((ctx,)), DMA((ctx,))],
        compiler_params=params(62, collective_id=2, has_side_effects=True), name="last",
    )(tbl, dq, dkv, h1, tok, wall, dx1, vec, gvec)


def shards(tokens, block_table, ln1_gain, ln1_bias, w_qkv, bias_query, bias_value, w_out, bias_out,
           ln2_gain, ln2_bias, w_up, bias_up, w_down, bias_down, cotangent):
    dp, ctx = lax.axis_size("dp"), lax.axis_size("ctx")
    width, hidden = tokens.shape[2], w_up.shape[1]
    r = w_qkv.shape[0]
    head = 128 + 3 * width
    third = (width + 2 * hidden) // 3
    off_up = head + width
    off_down = off_up + hidden
    small = jnp.concatenate([jnp.stack([ln1_gain, ln1_bias, bias_query, bias_value, bias_out, ln2_gain, ln2_bias,
                                        bias_down]), bias_up.reshape(4, r), jnp.zeros((116, r), BF)]).T
    cat = jnp.concatenate([small, w_qkv, w_out, w_up] + [w_down[j * r:(j + 1) * r] for j in range(4)], axis=1)
    tok_all, wall = gather(tokens[0], cat, dp, ctx, head, third)
    h1, q, kv, att, lse, vec = attend(block_table, tok_all, wall, ctx)
    bup = vec[8:12].reshape(4, dp, r).transpose(1, 0, 2).reshape(1, hidden)
    out, gt, da, dx1, delta, gvec, gup = feed_call(block_table, tokens[0], att, wall, cotangent[0], vec, bup,
                                                   ctx, off_up, off_down, 3 * third)
    dq, dkv = attend_back(block_table, q, kv, da, lse, delta, ctx)
    gvec = gvec.at[8:12].set(gup.reshape(dp, 4, r).transpose(1, 0, 2).reshape(4, width))
    gq, gtok = last_call(block_table, dq, dkv, h1, tokens[0], wall, dx1, vec, gvec, ctx, head)
    total = scatter(gq, gt, dp, ctx, head, third)
    rows = total[:, 0:128].T
    g_down = jnp.concatenate([total[:, off_down + j * width:off_down + (j + 1) * width] for j in range(4)], axis=0)
    return (out[None], gtok[None], rows[0], rows[1], total[:, 128:head], rows[2], rows[3],
            total[:, head:off_up], rows[4], rows[5], rows[6], total[:, off_up:off_down],
            rows[8:12].reshape(4 * r), g_down, rows[7])


def solution(mesh):
    row, mat = P("dp"), P("dp", None)
    act = P("dp", "ctx", None)
    in_specs = (act, P(), row, row, mat, row, row, mat, row, row, row, mat, row, mat, row, act)
    out_specs = (act, act, row, row, mat, row, row, mat, row, row, row, mat, row, mat, row)
    return jax.shard_map(shards, mesh=mesh, in_specs=in_specs, out_specs=out_specs, check_vma=False)
```

time: 862 us -> 367 us (0.43)
  waiting for transfers between devices: 360 us -> 0 us
  Pallas kernels: 0 us -> 327 us
  matrix products: 234 us -> 0 us
  blocking collectives: 129 us -> 0 us
  local copies, waits for them, and re-layouts: 74.3 us -> 32.6 us
  other arithmetic: 38.5 us -> 2.24 us
  between operations: 17.1 us -> 0.74 us
    pallas_call x0 -> x6, Pallas kernels: none -> 327 us  [the longest x1 107 us: scatter(): pl.pallas_call(functools.partial(scatter_kernel, dp, ctx, head, third), o...]
    dot_general x54 -> x0, matrix products: 234 us -> none  [the longest x6 43.1 us: backward_pair(): jnp.einsum('hts,shd->thd', grad_scores, key_part, preferred_element_type=...]
    reduce_scatter x5 -> x0, waiting for transfers between devices: 219 us -> none  [the longest x1 78.7 us: shards(): lax.psum_scatter(grad_down_w.astype(jnp.bfloat16), 'dp', scatter_dimensio...]
    unnamed x2 -> x0, blocking collectives: 124 us -> none
    all_gather x5 -> x0, waiting for transfers between devices: 111 us -> none  [the longest x1 46.7 us: shards(): lax.all_gather(w_down, 'dp', axis=0, tiled=True)]
    psum x1 -> x0, waiting for transfers between devices: 28.4 us -> none  [shards(): lax.psum(sum_qkv_w.astype(jnp.bfloat16), 'ctx').astype(jnp.float32)]
    dynamic_slice x43 -> x0, local copies, waits for them, and re-layouts: 24.8 us -> none  [the longest x6 6.49 us: pair_scores(): lax.dynamic_slice_in_dim(keyvals, pair_index * pair_width, pair_width, 1)]
    reduce_sum x14 -> x0, other arithmetic: 15.5 us -> none  [the longest x6 6.97 us: forward_pair(): row_total = jnp.sum(exponent, axis=-1, keepdims=True)]
  transfers between devices with their start and end apart: 11 -> 0, of which waited for: 8 -> 0; matrix products, arithmetic and copies ran while one was open for 15% -> 0% of each run, Pallas kernels for 0% -> 0%
where the time goes in v1:
time: 367 us; the launch traced here: 363 us
  Pallas kernels  327 us (89%)
  local copies, waits for them, and re-layouts  32.6 us (9%)
    pallas_call x1, Pallas kernels, scatter(): pl.pallas_call(functools.partial(scatter_kernel, dp, ctx, head, third), o...  107 us
    pallas_call x1, Pallas kernels, gather(): pl.pallas_call(functools.partial(gather_kernel, dp, ctx, head, third), ou...  85.1 us
    pallas_call x1, Pallas kernels, last_call(): pl.pallas_call(functools.partial(last_kernel, ctx), out_shape=(shape(dp,...  50.7 us
    pallas_call x1, Pallas kernels, feed_call(): pl.pallas_call(functools.partial(feed_kernel, ctx, dp // 4, off_up, off_d...  33.1 us
    pallas_call x1, Pallas kernels, attend_back(): pl.pallas_call(functools.partial(attend_back_kernel, ctx), out_shape=(sha...  26.7 us
    pallas_call x1, Pallas kernels, attend(): pl.pallas_call(functools.partial(attend_kernel, ctx), out_shape=(shape(ro...  24.4 us
    unnamed x16, local copies, waits for them, and re-layouts  13.7 us

profile of v1, /device:TPU:0, one launch (start us, length us, event | category | flops | bytes accessed | tf_op | source)
XLA Modules:
  0.0 363.0 jit_solution(7120862469461725740)
XLA Ops:
  0.6 0.7 reshape.74
  1.4 0.1 copy.49
  1.5 0.8 copy.41
  2.3 0.8 copy.42
  3.0 0.8 copy.43
  3.8 0.8 copy.44
  4.5 0.8 copy.45
  5.3 0.8 copy.46
  6.0 0.8 copy.47
  6.8 0.8 copy.48
  7.6 0.1 concatenate.11
  7.7 1.0 constant_dynamic-update-slice_fusion.2
  8.6 0.9 constant_dynamic-update-slice_fusion.1
  9.5 1.0 constant_dynamic-update-slice_fusion
  10.5 0.9 slice_dynamic-update-slice_fusion.3
  11.4 0.9 slice_dynamic-update-slice_fusion.2
  12.3 0.9 slice_dynamic-update-slice_fusion.1
  13.2 0.9 slice_dynamic-update-slice_fusion.cat_ref
  14.1 1.1 copy-done.1
  15.2 85.1 %shard_map.271 = (bf16[2,512,768]{2,1,0:T(8,128)(2,1)S(1)}, bf16[16,48,9344]{2,1,0:T(8,128)(2,1)S(1)}) custom-call(bf16[512,768]{1,0:T(8,128)(2,1)S(1)} %bitcast.24, bf16[48,9344]{1,0:T(8,128)(2,1)S(1)} %slice_dynamic-update-slice_fusion.cat_ref), custom_call_target="tpu_custom_call" | custom-call | tf_op jit(solution)/shard_map/pallas_call | solution.py:167
  100.3 0.0 copy-start
  100.3 5.1 %copy-done = bf16[16,48,9344]{2,1,0:T(8,128)(2,1)} copy-done((bf16[16,48,9344]{2,1,0:T(8,128)(2,1)}, bf16[16,48,9344]{2,1,0:T(8,128)(2,1)S(1)}, u32[]{:S(2)}) %copy-start) | copy-done | bytes 14352408
  105.4 1.1 copy-done.2
  106.5 24.4 %attend.1 = (bf16[512,768]{1,0:T(8,128)(2,1)}, bf16[512,768]{1,0:T(8,128)(2,1)}, bf16[1024,1536]{1,0:T(8,128)(2,1)}, bf16[2,256,768]{2,1,0:T(8,128)(2,1)}, f32[2,16,256]{2,1,0:T(8,128)}, /*index=5*/f32[16,768]{1,0:T(8,128)}) custom-call(s32[4]{0:T(128)} %tbl.7, bf16[2,512,768]{2,1,0:T(8,128)(2,1)} %copy-done.2, bf16[16,48,9344]{2,1,0:T(8,128)(2,1)} %copy-done), custom_call_target="tpu_custom_call" | custom-call | tf_op jit(solution)/shard_map/attend/pallas_call | solution.py:589
  130.9 0.7 slice.87
  131.7 0.1 reshape.75
  131.8 0.7 reshape.76.bup
  132.5 33.1 %feed.1 = (bf16[512,768]{1,0:T(8,128)(2,1)}, bf16[16,48,6912]{2,1,0:T(8,128)(2,1)}, bf16[512,768]{1,0:T(8,128)(2,1)}, f32[512,768]{1,0:T(8,128)}, f32[2,16,256]{...) custom-call(s32[4]{0:T(128)} %tbl.7, bf16[512,768]{1,0:T(8,128)(2,1)} %bitcast.22, ...), custom_call_target="tpu_custom_call" | custom-call | tf_op jit(solution)/shard_map/feed/pallas_call | solution.py:607
  165.6 0.5 broadcast.26
  166.1 1.4 reduce.21
  167.5 0.1 reshape.77
  167.6 0.1 reshape.78
  167.6 0.6 constant_dynamic-update-slice_fusion.4.gvec
  168.3 26.7 %attend_back.1 = (bf16[2,256,768]{2,1,0:T(8,128)(2,1)}, bf16[1024,1536]{1,0:T(8,128)(2,1)}) custom-call(s32[4]{0:T(128)} %tbl.7, bf16[512,768]{1,0:T(8,128)(2,1)} %get-tuple-element.51.q, bf16[1024,1536]{1,0:T(8,128)(2,1)} %get-tuple-element.52.kv, bf16[512,768]{1,0:T(8,128)(2,1)} %get-tuple-element.53.da, f32[2,16,256]{2,1,0:T(8,128)} %get-tuple-element.54.lse, ...), custom_call_target="tpu_custom_call" | custom-call | tf_op jit(solution)/shard_map/attend_back/pallas_call | solution.py:635
  195.0 50.7 %last.1 = (bf16[16,48,2432]{2,1,0:T(8,128)(2,1)}, bf16[512,768]{1,0:T(8,128)(2,1)}) custom-call(s32[4]{0:T(128)} %tbl.7, bf16[2,256,768]{2,1,0:T(8,128)(2,1)} %get-tuple-element.56.dq, bf16[1024,1536]{1,0:T(8,128)(2,1)} %get-tuple-element.57.dkv, bf16[512,768]{1,0:T(8,128)(2,1)} %get-tuple-element.58.h1, bf16[512,768]{1,0:T(8,128)(2,1)} %bitcast.23, ...), custom_call_target="tpu_custom_call" | custom-call | tf_op jit(solution)/shard_map/last/pallas_call | solution.py:674
  245.7 107.5 %shard_map.272 = f32[48,9344]{1,0:T(8,128)} custom-call(bf16[16,48,2432]{2,1,0:T(8,128)(2,1)} %get-tuple-element.63.gq, bf16[16,48,6912]{2,1,0:T(8,128)(2,1)} %get-tuple-element.64.gt), custom_call_target="tpu_custom_call" | custom-call | tf_op jit(solution)/shard_map/pallas_call | solution.py:306
  353.2 0.0 copy-start.3
  353.2 2.0 fusion
  355.2 0.9 pad_maximum_fusion
  356.0 1.9 slice.98
  357.9 1.8 slice.91
  359.7 0.7 slice_bitcast_fusion
  360.5 0.1 slice.112
  360.5 0.1 copy.52
  360.6 0.7 reshape.79
  361.3 0.8 slice_reduce_fusion
  362.1 0.0 copy-done.3
  362.1 0.9 copy.66
  (6 shorter events, 0.0 us)
Async XLA Ops:
  14.1 1.1 copy-start.1
  100.3 5.1 %copy-start = (bf16[16,48,9344]{2,1,0:T(8,128)(2,1)}, bf16[16,48,9344]{2,1,0:T(8,128)(2,1)S(1)}, u32[]{:S(2)}) copy-start(bf16[16,48,9344]{2,1,0:T(8,128)(2,1)S(1)} %get-tuple-element.47.wall) | copy-start | bytes 43057156
  105.4 1.1 copy-start.2
  353.2 8.9 %copy-start.3 = (bf16[512,768]{1,0:T(8,128)(2,1)S(1)}, bf16[512,768]{1,0:T(8,128)(2,1)}, u32[]{:S(2)}) copy-start(bf16[512,768]{1,0:T(8,128)(2,1)} %get-tuple-element.62) | copy-start | bytes 2359300

commit v2 on v1

--- a/solution.py
+++ b/solution.py
@@ -348,20 +348,25 @@
 
 
 class Table:
-    def __init__(self, tbl, nb, y):
+    def __init__(self, tbl, nb, y, ordered=False):
         self.nb, self.half = nb, nb // 2
         self.own = [tbl[2 * y], tbl[2 * y + 1]]
-        first_high = (self.own[0] >= self.half).astype(jnp.int32)
+        self.turned = self.own[0] >= self.half
+        first_high = self.turned.astype(jnp.int32)
+        self.place = [first_high, 1 - first_high]
         self.row_of = [first_high, 1 - first_high]
         self.slot_of = [first_high, 1 - first_high]
         self.block = [jnp.minimum(self.own[0], self.own[1]), jnp.maximum(self.own[0], self.own[1])]
+        self.tbl = tbl
+        if ordered:
+            self.row_of, self.slot_of, self.pos = [0, 1], [0, 1], list(range(nb))
+            return
         self.pos = []
         for j in range(nb):
             at = jnp.int32(0)
             for p in range(nb):
                 at = at + jnp.where(tbl[p] == j, p, 0)
             self.pos.append(at)
-        self.tbl = tbl
 
     def keys(self, slot):
         return self.half if slot == 0 else self.nb
@@ -375,12 +380,16 @@
     return value.reshape(value.shape[0] * value.shape[1], value.shape[2])
 
 
+def block_rows(i):
+    return pl.ds(i * BLK if isinstance(i, int) else pl.multiple_of(i * BLK, BLK), BLK)
+
+
 def lane_masks(rows):
     lane = lax.broadcasted_iota(jnp.int32, (rows, LANES), 1)
     return [lane < HD, lane >= HD]
 
 
-def project(ctx, tok, wall, h1, q, kv, vec, y):
+def project(ctx, table, tok, wall, h1, q, kv, vec, y, ordered=None):
     gain, shift = vec[0:1], vec[1:2]
     width = tok.shape[2]
     zero = jnp.zeros((1, width), F32)
@@ -390,7 +399,7 @@
     def rows(r, carry):
         x = tok[r // 2, pl.ds(pl.multiple_of((r % 2) * BLK, BLK), BLK)].astype(F32)
         low = (normed(x)[0] * gain + shift).astype(BF)
-        kv[pl.ds(pl.multiple_of(r * BLK, BLK), BLK)] = (dot(low, w_kv) + kv_bias).astype(BF)
+        kv[block_rows(r if ordered is None else table.tbl[r])] = (dot(low, w_kv) + kv_bias).astype(BF)
         return carry
 
     lax.fori_loop(0, 2 * ctx, rows, 0)
@@ -399,7 +408,14 @@
     def own(i, carry):
         at = pl.ds(pl.multiple_of(i * BLK, BLK), BLK)
         low = (normed(tok[y, at].astype(F32))[0] * gain + shift).astype(BF)
-        h1[at] = low
+        if ordered is None:
+            h1[at] = low
+        else:
+            cot, tok_slots, cot_slots = ordered
+            at, stored = block_rows(jnp.where(i == 0, table.place[0], table.place[1])), at
+            h1[:, at] = jnp.transpose(low)
+            tok_slots[at] = tok[y, stored]
+            cot_slots[at] = cot[stored]
         q[at] = ((dot(low, w_q) + vec[2:3]).astype(BF).astype(F32) * HD ** (-0.5)).astype(BF)
         return carry
 
@@ -412,8 +428,8 @@
     masks = lane_masks(BLK)
     lane = lax.broadcasted_iota(jnp.int32, (BLK, LANES), 1)
     for slot in range(2):
-        q2 = q[pl.ds(pl.multiple_of(table.row_of[slot] * BLK, BLK), BLK), lanes]
-        spots = [pl.ds(pl.multiple_of(table.pos[j] * BLK, BLK), BLK) for j in range(table.keys(slot))]
+        q2 = q[block_rows(table.row_of[slot]), lanes]
+        spots = [block_rows(table.pos[j]) for j in range(table.keys(slot))]
         mixed = []
         for h in range(2):
             qm = jnp.where(masks[h], q2, jnp.zeros_like(q2))
@@ -433,12 +449,12 @@
         att[slot, :, lanes] = jnp.where(masks[0], mixed[0], mixed[1]).astype(BF)
 
 
-def attend_back_pair(hp, table, q, kv, da, lse, delta, dq, dk_acc, dv_acc, width):
+def attend_back_pair(hp, table, q, kv, da, lse, delta, put_dq, dk_acc, dv_acc, width):
     lanes = pl.ds(pl.multiple_of(hp * LANES, LANES), LANES)
     v_lanes = pl.ds(pl.multiple_of(width + hp * LANES, LANES), LANES)
     masks = lane_masks(BLK)
     for slot in (1, 0):
-        row = pl.ds(pl.multiple_of(table.row_of[slot] * BLK, BLK), BLK)
+        row = block_rows(table.row_of[slot])
         q2, da2 = q[row, lanes], da[row, lanes]
         dq_acc = None
         for h in range(2):
@@ -447,7 +463,7 @@
             lse_row = lse[slot, pl.ds(2 * hp + h, 1), :]
             delta_row = delta[table.row_of[slot], pl.ds(2 * hp + h, 1), :]
             for j in range(table.keys(slot)):
-                at = pl.ds(pl.multiple_of(table.pos[j] * BLK, BLK), BLK)
+                at = block_rows(table.pos[j])
                 k2, v2 = kv[at, lanes], kv[at, v_lanes]
                 st = dot_t(k2, qm)
                 if table.masked(slot, j):
@@ -462,7 +478,7 @@
                     dk_acc[j] += dk
                 part = dot_l(dst, jnp.where(masks[h], k2, jnp.zeros_like(k2)))
                 dq_acc = part if dq_acc is None else dq_acc + part
-        dq[slot, :, lanes] = (dq_acc * HD ** (-0.5)).astype(BF)
+        put_dq(slot, (dq_acc * HD ** (-0.5)).astype(BF))
 
 
 def feed(nd, off_up, off_down, table, tok, att, wall, cot, vec, bup, out, gt, da, dx1, delta, gvec, gup,
@@ -566,13 +582,17 @@
     return jax.ShapeDtypeStruct(dims, dtype)
 
 
-def attend_kernel(ctx, tbl, tok, wall, h1, q, kv, att, lse, vec, lse_acc):
+def attend_kernel(ctx, ordered, tbl, tok, wall, *rest):
     width = tok.shape[2]
     y = lax.axis_index("ctx")
-    table = Table(tbl, 2 * ctx, y)
+    table = Table(tbl, 2 * ctx, y, ordered)
+    extra = None
+    if ordered:
+        extra, rest = (rest[0], *rest[1:3]), rest[3:]
+    h1, q, kv, att, lse, vec, lse_acc = rest
     small = rows_of(wall, slice(None), slice(None), slice(0, 128)).astype(F32)
     vec[...] = jnp.transpose(small)[0:16]
-    project(ctx, tok, wall, h1, q, kv, vec, y)
+    project(ctx, table, tok, wall, h1, q, kv, vec, y, extra)
     lse_acc[...] = jnp.zeros_like(lse_acc)
 
     def pair(hp, carry):
@@ -584,16 +604,19 @@
         lse[slot] = jnp.transpose(lse_acc[slot])[0:16]
 
 
-def attend(tbl, tok_all, wall, ctx):
+def attend(tbl, tok_all, wall, ctx, cot=None):
     rows, width = tok_all.shape[1:]
+    ordered = cot is not None
+    slots = (shape(rows, width), shape(rows, width), shape(width, rows)) if ordered else (shape(rows, width),)
+    outs = slots + (shape(rows, width), shape(ctx * rows, 2 * width), shape(2, BLK, width),
+                    shape(2, 16, BLK, dtype=F32), shape(16, width, dtype=F32))
+    args = (tbl, tok_all, wall) + ((cot,) if ordered else ())
     return pl.pallas_call(
-        functools.partial(attend_kernel, ctx),
-        out_shape=(shape(rows, width), shape(rows, width), shape(ctx * rows, 2 * width), shape(2, BLK, width),
-                   shape(2, 16, BLK, dtype=F32), shape(16, width, dtype=F32)),
-        in_specs=[SM, VM, VM], out_specs=(VM,) * 6,
+        functools.partial(attend_kernel, ctx, ordered),
+        out_shape=outs, in_specs=[SM] + [VM] * (len(args) - 1), out_specs=(VM,) * len(outs),
         scratch_shapes=[pltpu.VMEM((2, BLK, LANES), F32)],
         compiler_params=params(62), name="attend",
-    )(tbl, tok_all, wall)
+    )(*args)
 
 
 def feed_kernel(ctx, nd, off_up, off_down, tbl, tok, att, wall, cot, vec, bup, *rest):
@@ -620,7 +643,10 @@
     table = Table(tbl, 2 * ctx, lax.axis_index("ctx"))
 
     def pair(hp, carry):
-        attend_back_pair(hp, table, q, kv, da, lse, delta, dq, dk_acc, dv_acc, width)
+        def put_dq(slot, value):
+            dq[slot, :, pl.ds(pl.multiple_of(hp * LANES, LANES), LANES)] = value
+
+        attend_back_pair(hp, table, q, kv, da, lse, delta, put_dq, dk_acc, dv_acc, width)
         for j in range(2 * ctx):
             at = pl.ds(pl.multiple_of(table.pos[j] * BLK, BLK), BLK)
             dkv[at, pl.ds(pl.multiple_of(hp * LANES, LANES), LANES)] = dk_acc[j].astype(BF)
@@ -680,6 +706,378 @@
     )(tbl, dq, dkv, h1, tok, wall, dx1, vec, gvec)
 
 
+class Reduce:
+    def __init__(self, at, g, a_core, a_x, a_z, a_y, sems):
+        self.at, self.g = at, g
+        self.a_core, self.a_x, self.a_z, self.a_y = a_core, a_x, a_z, a_y
+        self.s1, self.r1, self.s2, self.r2, self.s3, self.r3, self.s4, self.r4 = sems
+        self.mate = {"dp": at.dp_at(at.z, at.x, 1 - at.c)}
+        self.across = {"dp": at.dp_at(at.z, 1 - at.x, at.c)}
+
+    def to_core(self, p, cols, held=None):
+        return remote(self.g.at[:, :, 1 - self.at.c, :, cols if held is None else held], self.a_core.at[:, :, :, cols],
+                      self.s1.at[p], self.r1.at[p], self.mate)
+
+    def to_x(self, p, cols):
+        return remote(self.a_core.at[:, 1 - self.at.x, :, cols], self.a_x.at[:, :, cols],
+                      self.s2.at[p], self.r2.at[p], self.across)
+
+    def to_z(self, p, cols, k):
+        at = self.at
+        return remote(self.a_core.at[at.z_at(k), at.x, :, cols], self.a_z.at[k - 1, :, cols],
+                      self.s3.at[p, k - 1], self.r3.at[p, k - 1], {"dp": at.dp_at(at.z_at(k), at.x, at.c)})
+
+    def to_y(self, p, cols, k):
+        at = self.at
+        return remote(self.a_core.at[at.z, at.x, :, cols], self.a_y.at[k - 1, :, cols],
+                      self.s4.at[p, k - 1], self.r4.at[p, k - 1], {"ctx": at.y_at(k)})
+
+    def level1(self, p, cols, held=None):
+        self.to_core(p, cols, held).start()
+
+    def level2(self, p, cols, held=None):
+        self.to_core(p, cols, held).wait_recv()
+        own = self.g[:, :, self.at.c, :, cols if held is None else held]
+        self.a_core[:, :, :, cols] = self.a_core[:, :, :, cols] + own
+        self.to_x(p, cols).start()
+
+    def level3(self, p, cols):
+        at = self.at
+        self.to_x(p, cols).wait_recv()
+        self.a_core[:, at.x, :, cols] = self.a_core[:, at.x, :, cols] + self.a_x[:, :, cols]
+        for k in near_first(at.lines):
+            self.to_z(p, cols, k).start()
+
+    def level4(self, p, cols):
+        at = self.at
+        total = self.a_core[at.z, at.x, :, cols].astype(F32)
+        for k in near_first(at.lines):
+            self.to_z(p, cols, k).wait_recv()
+            total = total + self.a_z[k - 1, :, cols].astype(F32)
+        self.a_core[at.z, at.x, :, cols] = total.astype(BF)
+        for k in range(1, at.ctx):
+            self.to_y(p, cols, k).start()
+
+    def level5(self, p, cols):
+        at = self.at
+        total = self.a_core[at.z, at.x, :, cols].astype(F32)
+        for k in range(1, at.ctx):
+            self.to_y(p, cols, k).wait_recv()
+            total = total + self.a_y[k - 1, :, cols].astype(F32)
+        return total
+
+    def finish(self, p, cols, core=True, held=None):
+        at = self.at
+        if core:
+            self.to_core(p, cols, held).wait_send()
+        self.to_x(p, cols).wait_send()
+        for k in range(1, at.lines):
+            self.to_z(p, cols, k).wait_send()
+        for k in range(1, at.ctx):
+            self.to_y(p, cols, k).wait_send()
+
+
+def backward_kernel(dp, ctx, tbl, tok, att, cot, q, kv, h1t, lse, vec, bup, wall,
+                    out, gtok, o_small, o_qkv, o_out, o_up, o_down,
+                    x1, acc, dh2, da, delta, dq, dk_acc, dv_acc, send, recv, dqkv, gup, rows,
+                    wub, wdb, g, a_core, a_x, a_z, a_y, wsem, ys, yr, *sems):
+    at = Spot(dp, ctx)
+    width = tok.shape[1]
+    r = wall.shape[1]
+    nd = dp // 4
+    chunk = 4 * nd * r
+    off_out = 128 + 3 * width
+    off_up = off_out + width
+    off_down = off_up + 4 * chunk
+    table = Table(tbl, 2 * ctx, at.y, True)
+    red = Reduce(at, g, a_core, a_x, a_z, a_y, sems)
+    lines = at.lines
+    last_t = 9
+    actb, dub, h2 = dqkv.at[0], dqkv.at[1], dqkv.at[2]
+
+    def cols_of(p):
+        return pl.ds(pl.multiple_of(p * width, 128), width)
+
+    def cols_q(hp):
+        return pl.ds(pl.multiple_of(last_t * width + hp * 3 * LANES, 128), 3 * LANES)
+
+    def held_q(hp):
+        return pl.ds(pl.multiple_of(last_t * width + 128 + lax.rem(hp, 3) * 3 * LANES, 128), 3 * LANES)
+
+    cols_small = pl.ds(last_t * width + 3 * width, 128)
+    held_small = pl.ds(last_t * width, 128)
+
+    def up_copy(f, slot):
+        return pltpu.make_async_copy(wall.at[:, :, pl.ds(pl.multiple_of(off_up + f * chunk, 128), chunk)],
+                                     wub.at[slot], wsem.at[0, slot])
+
+    def down_copy(f, slot, j):
+        return pltpu.make_async_copy(wall.at[pl.ds(f * nd, nd), :, pl.ds(off_down + j * width, width)],
+                                     wdb.at[slot, :, j], wsem.at[1 + j, slot])
+
+    def plain_copy(i, slot):
+        return pltpu.make_async_copy(wall.at[:, :, pl.ds(128 + i * width, width)], wub.at[slot], wsem.at[5, slot])
+
+    def fetch(f, slot):
+        up_copy(f, slot).start()
+        for j in range(4):
+            down_copy(f, slot, j).start()
+
+    plain_copy(3, 2).start()
+    fetch(0, 0)
+    at.barrier()
+    plain_copy(3, 2).wait()
+    w_out = wub[2].reshape(width, width)
+    halves = [pl.ds(i * BLK, BLK) for i in range(2)]
+    for i, half in enumerate(halves):
+        mid = tok[half].astype(F32) + (dot(att[table.slot_of[i]], w_out) + vec[4:5])
+        x1[half] = mid
+        low = (normed(mid)[0] * vec[5:6] + vec[6:7]).astype(BF)
+        h2[half] = low
+        acc[half] = mid + vec[7:8]
+        dh2[half] = jnp.zeros((BLK, width), F32)
+
+    def part(f, carry):
+        slot = lax.rem(f, 2)
+
+        @pl.when(f < 3)
+        def _():
+            fetch(f + 1, 1 - slot)
+
+        up_copy(f, slot).wait()
+        for j in range(4):
+            down_copy(f, slot, j).wait()
+        w_up = wub[slot].reshape(width, chunk)
+        w_down = wdb[slot].reshape(chunk, width)
+        hid = pl.ds(pl.multiple_of(f * chunk, 128), chunk)
+        bias = bup[:, hid]
+        sums = jnp.zeros((1, chunk), F32)
+        for half in halves:
+            u = dot(h2[half], w_up) + bias
+            sq = u * u
+            t = jnp.tanh(u * (0.7978845608028654 + 0.03567740813636141 * sq))
+            act = (0.5 * u * (1.0 + t)).astype(BF)
+            actb[half] = act
+            slope = 0.5 * (1.0 + t) + 0.5 * u * (1.0 - t * t) * (0.7978845608028654 + 0.10703222440908423 * sq)
+            acc[half] += dot(act, w_down)
+            dul = (slope * dot_t(cot[half], w_down)).astype(BF)
+            dub[half] = dul
+            sums = sums + jnp.sum(dul.astype(F32), axis=0, keepdims=True)
+            dh2[half] += dot_t(dul, w_up)
+        gup[:, hid] = sums
+        g[:, :, :, :, cols_of(f)] = dot_l(h2[...], dub[...]).astype(BF).reshape(lines, 2, 2, r, chunk)
+        red.level1(f, cols_of(f))
+        g_down = dot_l(actb[...], cot[...]).astype(BF).reshape(nd // 4, 2, 2, 4, r, width)
+        for j in range(4):
+            g[pl.ds(f * (nd // 4), nd // 4), :, :, :, pl.ds((4 + j) * width, width)] = g_down[:, :, :, j]
+        for lag, level in ((1, red.level2), (2, red.level3), (3, red.level4)):
+            @pl.when(f >= lag)
+            def _():
+                level(f - lag, cols_of(f - lag))
+        return carry
+
+    lax.fori_loop(0, 4, part, 0)
+    for p in range(4, 8):
+        red.level1(p, cols_of(p))
+    for i, half in enumerate(halves):
+        out[half] = jnp.where(table.turned, acc[halves[1 - i]], acc[half]).astype(BF)
+    rows[...] = jnp.zeros_like(rows)
+    lane_head = lax.broadcasted_iota(jnp.int32, (16, width), 0)
+    pick = (lax.broadcasted_iota(jnp.int32, (16, width), 1) // HD == lane_head).astype(F32)
+    grad = None
+    w_out = wub[2].reshape(width, width)
+    for i, half in enumerate(halves):
+        gf = cot[half].astype(F32)
+        unit, inv = normed(x1[half])
+        dy = dh2[half]
+        mid_grad = gf + norm_back(dy, unit, inv, vec[5:6])
+        acc[half] = mid_grad
+        branch = mid_grad.astype(BF)
+        rows[4:5] += jnp.sum(branch.astype(F32), axis=0, keepdims=True)
+        rows[5:6] += jnp.sum(dy * unit, axis=0, keepdims=True)
+        rows[6:7] += jnp.sum(dy, axis=0, keepdims=True)
+        rows[7:8] += jnp.sum(gf, axis=0, keepdims=True)
+        own = att[table.slot_of[i]]
+        piece = dot_l(own, branch)
+        grad = piece if grad is None else grad + piece
+        back = dot_t(branch, w_out).astype(BF)
+        da[half] = back
+        delta[i] = lax.dot_general(pick, back.astype(F32) * own.astype(F32), (((1,), (1,)), ((), ())),
+                                   precision=lax.Precision.HIGHEST, preferred_element_type=F32)
+    g[:, :, :, :, cols_of(8)] = grad.astype(BF).reshape(lines, 2, 2, r, width)
+    red.level1(8, cols_of(8))
+    for i in range(3):
+        plain_copy(i, i).start()
+    red.level2(3, cols_of(3))
+    red.level3(2, cols_of(2))
+    red.level4(1, cols_of(1))
+
+    def done_t(p):
+        total = red.level5(p, cols_of(p))
+
+        @pl.when(p < 4)
+        def _():
+            o_up[:, pl.ds(pl.multiple_of(jnp.minimum(p, 3) * width, 128), width)] = total
+
+        @pl.when(p >= 4)
+        def _():
+            o_down[pl.ds(pl.multiple_of(jnp.clip(p - 4, 0, 3) * r, 8), r), :] = total
+
+    done_t(jnp.int32(0))
+    other = lax.rem(at.y + 1, 2)
+    mate_y = {"ctx": other}
+
+    def kv_copy(hp):
+        return remote(send.at[hp], recv.at[hp], ys.at[hp], yr.at[hp], mate_y)
+
+    def q_grad(hp):
+        lanes = pl.ds(pl.multiple_of(hp * LANES, LANES), LANES)
+        kv_copy(hp).wait_recv()
+        for i in range(2):
+            dqkv[1 + i, :, lanes] = (dqkv[1 + i, :, lanes].astype(F32)
+                                     + recv[hp, :, i * LANES:(i + 1) * LANES].astype(F32)).astype(BF)
+        low = jnp.concatenate([dqkv[i, :, lanes] for i in range(3)], axis=1)
+
+        @pl.when(hp >= 3)
+        def _():
+            red.to_core(last_t + jnp.maximum(hp - 3, 0), cols_q(0), held_q(0)).wait_send()
+
+        g[:, :, :, :, held_q(hp)] = dot(h1t[...], low).astype(BF).reshape(lines, 2, 2, r, 3 * LANES)
+        red.level1(last_t + hp, cols_q(hp), held_q(hp))
+
+    def done_q(hp):
+        total = red.level5(last_t + hp, cols_q(hp))
+        for i in range(3):
+            o_qkv[:, pl.ds(pl.multiple_of(i * width + hp * LANES, LANES), LANES)] = total[:, i * LANES:(i + 1) * LANES]
+
+    def level_q(level, hp):
+        if level == red.level2:
+            level(last_t + hp, cols_q(hp), held_q(hp))
+        else:
+            level(last_t + hp, cols_q(hp))
+
+    outermost = table.block[0] == 0
+
+    def pair(hp, carry):
+        def put_dq(slot, value):
+            dq[slot] = value
+
+        attend_back_pair(hp, table, q, kv, da, lse, delta, put_dq, dk_acc, dv_acc, width)
+        lanes = pl.ds(pl.multiple_of(hp * LANES, LANES), LANES)
+        for i, half in enumerate(halves):
+            dqkv[0, half, lanes] = dq[i]
+            outer, inner = (0, 1) if i == 0 else (3, 2)
+            for n, sums in enumerate((dk_acc, dv_acc)):
+                dqkv[1 + n, half, lanes] = jnp.where(outermost, sums[outer], sums[inner]).astype(BF)
+                send[hp, half, n * LANES:(n + 1) * LANES] = jnp.where(outermost, sums[inner], sums[outer]).astype(BF)
+        kv_copy(hp).start()
+
+        @pl.when(hp < 5)
+        def _():
+            red.level2(4 + hp, cols_of(4 + hp))
+
+        red.level3(3 + hp, cols_of(3 + hp))
+        red.level4(2 + hp, cols_of(2 + hp))
+        done_t(1 + hp)
+
+        @pl.when(hp >= 2)
+        def _():
+            q_grad(hp - 2)
+
+        for lag, level in ((3, red.level2), (4, red.level3), (5, red.level4)):
+            @pl.when(hp >= lag)
+            def _():
+                level_q(level, hp - lag)
+        return carry
+
+    lax.fori_loop(0, PAIRS, pair, 0)
+    for i in range(3):
+        plain_copy(i, i).wait()
+    red.level4(8, cols_of(8))
+    done_t(jnp.int32(7))
+    q_grad(jnp.int32(4))
+    level_q(red.level2, 3)
+    level_q(red.level3, 2)
+    level_q(red.level4, 1)
+    o_out[...] = red.level5(8, cols_of(8))
+    done_q(0)
+    q_grad(jnp.int32(5))
+    level_q(red.level2, 4)
+    level_q(red.level3, 3)
+    level_q(red.level4, 2)
+    done_q(1)
+    for i in range(3):
+        piece = dot_t(dqkv[i], wub[i].reshape(width, width))
+        if i == 0:
+            dh2[...] = piece
+        else:
+            dh2[...] += piece
+    level_q(red.level2, 5)
+    level_q(red.level3, 4)
+    level_q(red.level4, 3)
+    for half in halves:
+        dy = dh2[half]
+        unit, inv = normed(tok[half].astype(F32))
+        acc[half] += norm_back(dy, unit, inv, vec[0:1])
+        rows[0:1] += jnp.sum(dy * unit, axis=0, keepdims=True)
+        rows[1:2] += jnp.sum(dy, axis=0, keepdims=True)
+        rows[2:3] += jnp.sum(dqkv[0, half].astype(F32), axis=0, keepdims=True)
+        rows[3:4] += jnp.sum(dqkv[2, half].astype(F32), axis=0, keepdims=True)
+    for i, half in enumerate(halves):
+        gtok[half] = jnp.where(table.turned, acc[halves[1 - i]], acc[half]).astype(BF)
+    small = jnp.transpose(rows[...])
+    lane = lax.broadcasted_iota(jnp.int32, small.shape, 1)
+    tall = jnp.transpose(jnp.broadcast_to(gup[...], (8, 4 * chunk))).reshape(dp, 4, r, 8)
+    for j in range(4):
+        small = jnp.where(lane == 8 + j, tall[:, j].reshape(width, 8)[:, 0:1], small)
+    g[:, :, :, :, held_small] = small.astype(BF).reshape(lines, 2, 2, r, 128)
+    red.level1(last_t + 6, cols_small, held_small)
+    level_q(red.level3, 5)
+    red.level2(last_t + 6, cols_small, held_small)
+    level_q(red.level4, 4)
+    done_q(2)
+    done_q(3)
+    red.level3(last_t + 6, cols_small)
+    level_q(red.level4, 5)
+    red.level4(last_t + 6, cols_small)
+    done_q(4)
+    done_q(5)
+    o_small[...] = red.level5(last_t + 6, cols_small)
+    for p in range(last_t):
+        red.finish(p, cols_of(p))
+    for hp in range(PAIRS):
+        red.finish(last_t + hp, cols_q(hp), hp >= 3, held_q(hp))
+        kv_copy(hp).wait_send()
+    red.finish(last_t + 6, cols_small, True, held_small)
+
+
+def backward(tbl, tok, att, cot, q, kv, h1t, lse, vec, bup, wall, ctx):
+    rows, width = tok.shape
+    dp, r, full = wall.shape
+    lines, nd = dp // 4, dp // 4
+    chunk = 4 * nd * r
+    V = pltpu.VMEM
+    return pl.pallas_call(
+        functools.partial(backward_kernel, dp, ctx),
+        out_shape=(shape(rows, width), shape(rows, width), shape(r, 128, dtype=F32), shape(r, 3 * width, dtype=F32),
+                   shape(r, width, dtype=F32), shape(r, 4 * chunk, dtype=F32), shape(4 * r, width, dtype=F32)),
+        in_specs=[SM] + [VM] * 9 + [ANY], out_specs=(VM,) * 7,
+        scratch_shapes=[V((rows, width), F32), V((rows, width), F32), V((rows, width), F32), V((rows, width), BF),
+                        V((2, 16, BLK), F32),
+                        V((2, BLK, LANES), BF), V((2 * ctx, BLK, LANES), F32), V((2 * ctx, BLK, LANES), F32),
+                        V((PAIRS, rows, 2 * LANES), BF), V((PAIRS, rows, 2 * LANES), BF), V((3, rows, width), BF),
+                        V((1, 4 * chunk), F32), V((128, width), F32),
+                        V((3, dp, r, chunk), BF), V((2, nd, 4, r, width), BF),
+                        V((lines, 2, 2, r, 9 * width + 128 + 9 * LANES), BF), V((lines, 2, r, full), BF), V((lines, r, full), BF),
+                        V((lines - 1, r, full), BF), V((ctx - 1, r, full), BF),
+                        DMA((6, 3)), DMA((PAIRS,)), DMA((PAIRS,)),
+                        DMA((16,)), DMA((16,)), DMA((16,)), DMA((16,)), DMA((16, lines - 1)), DMA((16, lines - 1)),
+                        DMA((16, ctx - 1)), DMA((16, ctx - 1))],
+        compiler_params=pltpu.CompilerParams(vmem_limit_bytes=67043328, collective_id=3, has_side_effects=True),
+        name="backward",
+    )(tbl, tok, att, cot, q, kv, h1t, lse, vec, bup, wall)
+
+
 def shards(tokens, block_table, ln1_gain, ln1_bias, w_qkv, bias_query, bias_value, w_out, bias_out,
            ln2_gain, ln2_bias, w_up, bias_up, w_down, bias_down, cotangent):
     dp, ctx = lax.axis_size("dp"), lax.axis_size("ctx")
@@ -693,8 +1091,15 @@
                                         bias_down]), bias_up.reshape(4, r), jnp.zeros((116, r), BF)]).T
     cat = jnp.concatenate([small, w_qkv, w_out, w_up] + [w_down[j * r:(j + 1) * r] for j in range(4)], axis=1)
     tok_all, wall = gather(tokens[0], cat, dp, ctx, head, third)
-    h1, q, kv, att, lse, vec = attend(block_table, tok_all, wall, ctx)
+    fused = ctx == 2 and dp == 16
+    *slots, h1, q, kv, att, lse, vec = attend(block_table, tok_all, wall, ctx, cotangent[0] if fused else None)
     bup = vec[8:12].reshape(4, dp, r).transpose(1, 0, 2).reshape(1, hidden)
+    if fused:
+        out, gtok, g_small, g_qkv, g_out, g_up, g_down = backward(
+            block_table, slots[0], att, slots[1], q, kv, h1, lse, vec, bup, wall, ctx)
+        rows = g_small.T
+        return (out[None], gtok[None], rows[0], rows[1], g_qkv, rows[2], rows[3], g_out, rows[4], rows[5], rows[6],
+                g_up, rows[8:12].reshape(4 * r), g_down, rows[7])
     out, gt, da, dx1, delta, gvec, gup = feed_call(block_table, tokens[0], att, wall, cotangent[0], vec, bup,
                                                    ctx, off_up, off_down, 3 * third)
     dq, dkv = attend_back(block_table, q, kv, da, lse, delta, ctx)

time: 367 us -> 261 us (0.71)
  Pallas kernels: 327 us -> 226 us
    pallas_call x5 -> x2, Pallas kernels: 242 us -> 141 us  [the longest x1 117 us: backward(): pl.pallas_call(functools.partial(backward_kernel, dp, ctx), out_shape=(sh...]
    unnamed x16 -> x27, local copies, waits for them, and re-layouts: 13.7 us -> 20.1 us
    slice x3 -> x0, local copies, waits for them, and re-layouts: 5.7 us -> none  [the longest x1 1.98 us: shards(): total[:, off_down + j * width:off_down + (j + 1) * width]]
where the time goes in v2:
time: 261 us; the launch traced here: 260 us
  Pallas kernels  226 us (87%)
  local copies, waits for them, and re-layouts  33 us (13%)
    pallas_call x1, Pallas kernels, backward(): pl.pallas_call(functools.partial(backward_kernel, dp, ctx), out_shape=(sh...  117 us
    pallas_call x1, Pallas kernels, gather(): pl.pallas_call(functools.partial(gather_kernel, dp, ctx, head, third), ou...  85.1 us
    pallas_call x1, Pallas kernels, attend(): pl.pallas_call(functools.partial(attend_kernel, ctx, ordered), out_shape=...  24.1 us
    unnamed x27, local copies, waits for them, and re-layouts  20.1 us
    another operation x8, local copies, waits for them, and re-layouts, shards(): jnp.stack([ln1_gain, ln1_bias, bias_query, bias_value, bias_out, ln2_gain...  6.05 us

profile of v2, /device:TPU:0, one launch (start us, length us, event | category | flops | bytes accessed | tf_op | source)
XLA Modules:
  0.0 259.6 jit_solution(8263224604282065414)
XLA Ops:
  0.6 0.7 reshape.42
  1.4 0.1 copy.48
  1.5 0.8 copy.40
  2.3 0.8 copy.41
  3.0 0.8 copy.42
  3.8 0.8 copy.43
  4.5 0.8 copy.44
  5.3 0.8 copy.45
  6.0 0.8 copy.46
  6.8 0.8 copy.47
  7.6 0.1 concatenate.6
  7.7 1.0 constant_dynamic-update-slice_fusion.2
  8.6 0.9 constant_dynamic-update-slice_fusion.1
  9.5 1.0 constant_dynamic-update-slice_fusion
  10.5 0.9 slice_dynamic-update-slice_fusion.3
  11.4 0.9 slice_dynamic-update-slice_fusion.2
  12.3 0.9 slice_dynamic-update-slice_fusion.1
  13.2 0.9 slice_dynamic-update-slice_fusion.cat_ref
  14.1 0.0 copy-start.2
  14.1 1.1 copy-done.2
  15.2 85.1 %shard_map.271 = (bf16[2,512,768]{2,1,0:T(8,128)(2,1)S(1)}, bf16[16,48,9344]{2,1,0:T(8,128)(2,1)S(1)}) custom-call(bf16[512,768]{1,0:T(8,128)(2,1)S(1)} %bitcast.18, bf16[48,9344]{1,0:T(8,128)(2,1)S(1)} %slice_dynamic-update-slice_fusion.cat_ref), custom_call_target="tpu_custom_call" | custom-call | tf_op jit(solution)/shard_map/pallas_call | solution.py:167
  100.3 0.0 copy-start
  100.3 5.1 %copy-done = bf16[16,48,9344]{2,1,0:T(8,128)(2,1)} copy-done((bf16[16,48,9344]{2,1,0:T(8,128)(2,1)}, bf16[16,48,9344]{2,1,0:T(8,128)(2,1)S(1)}, u32[]{:S(2)}) %copy-start) | copy-done | bytes 14352408
  105.4 0.0 copy-start.1
  105.4 1.2 copy-done.1
  106.5 24.1 %attend.1 = (bf16[512,768]{1,0:T(8,128)(2,1)}, bf16[512,768]{1,0:T(8,128)(2,1)}, bf16[768,512]{1,0:T(8,128)(2,1)}, bf16[512,768]{1,0:T(8,128)(2,1)}, bf16[1024,1...) custom-call(s32[4]{0:T(128)} %tbl.3, ...), custom_call_target="tpu_custom_call" | custom-call | tf_op jit(solution)/shard_map/attend/pallas_call | solution.py:614
  130.6 0.7 slice.46
  131.4 0.1 reshape.43
  131.5 0.7 reshape.44.bup
  132.2 116.8 %backward.1 = (bf16[512,768]{1,0:T(8,128)(2,1)}, bf16[512,768]{1,0:T(8,128)(2,1)}, f32[48,128]{1,0:T(8,128)}, f32[48,2304]{1,0:T(8,128)}, f32[48,768]{1,0:T(8,12...) custom-call(s32[4]{0:T(128)} %tbl.3, bf16[512,768]{1,0:T(8,128)(2,1)} %get-tuple-element.34.tok, ...), custom_call_target="tpu_custom_call" | custom-call | tf_op jit(solution)/shard_map/backward/pallas_call | solution.py:1060
  249.0 0.0 copy-start.5
  249.0 0.0 copy-start.6
  249.0 0.0 copy-start.4
  249.0 0.0 copy-start.3
  249.0 1.9 slice_reduce_fusion
  250.9 0.8 slice.63
  251.7 0.1 copy.50
  251.8 0.7 reshape.45
  252.5 2.1 copy.66
  254.5 2.1 copy.67
  256.6 0.0 copy-done.5
  256.6 0.8 copy.68
  257.3 0.0 copy-done.6
  257.3 0.7 copy.69
  258.0 0.0 copy-done.4
  258.0 0.8 copy.70
  258.8 0.0 copy-done.3
  258.8 0.8 copy.71
  (3 shorter events, 0.0 us)
Async XLA Ops:
  14.1 1.1 copy-start.2
  100.3 5.1 %copy-start = (bf16[16,48,9344]{2,1,0:T(8,128)(2,1)}, bf16[16,48,9344]{2,1,0:T(8,128)(2,1)S(1)}, u32[]{:S(2)}) copy-start(bf16[16,48,9344]{2,1,0:T(8,128)(2,1)S(1)} %get-tuple-element.33.wall) | copy-start | bytes 43057156
  105.4 1.2 copy-start.1
  249.0 7.6 %copy-start.5 = (f32[48,2304]{1,0:T(8,128)S(1)}, f32[48,2304]{1,0:T(8,128)}, u32[]{:S(2)}) copy-start(f32[48,2304]{1,0:T(8,128)} %get-tuple-element.76) | copy-start | bytes 1327108
  249.0 8.3 %copy-start.6 = (f32[48,768]{1,0:T(8,128)S(1)}, f32[48,768]{1,0:T(8,128)}, u32[]{:S(2)}) copy-start(f32[48,768]{1,0:T(8,128)} %get-tuple-element.79) | copy-start | bytes 442372
  249.0 9.0 %copy-start.4 = (f32[48,3072]{1,0:T(8,128)S(1)}, f32[48,3072]{1,0:T(8,128)}, u32[]{:S(2)}) copy-start(f32[48,3072]{1,0:T(8,128)} %get-tuple-element.83) | copy-start | bytes 1769476
  249.0 9.8 %copy-start.3 = (f32[192,768]{1,0:T(8,128)S(1)}, f32[192,768]{1,0:T(8,128)}, u32[]{:S(2)}) copy-start(f32[192,768]{1,0:T(8,128)} %get-tuple-element.85) | copy-start | bytes 1769476

commit v3 on v2

--- a/solution.py
+++ b/solution.py
@@ -8,6 +8,7 @@
 
 ANY = pl.BlockSpec(memory_space=pl.ANY)
 VM = pl.BlockSpec(memory_space=pltpu.VMEM)
+HBM = pl.BlockSpec(memory_space=pltpu.HBM)
 DMA = pltpu.SemaphoreType.DMA
 
 
@@ -389,7 +390,7 @@
     return [lane < HD, lane >= HD]
 
 
-def project(ctx, table, tok, wall, h1, q, kv, vec, y, ordered=None):
+def project(ctx, tok, wall, h1, q, kv, vec, y):
     gain, shift = vec[0:1], vec[1:2]
     width = tok.shape[2]
     zero = jnp.zeros((1, width), F32)
@@ -399,7 +400,7 @@
     def rows(r, carry):
         x = tok[r // 2, pl.ds(pl.multiple_of((r % 2) * BLK, BLK), BLK)].astype(F32)
         low = (normed(x)[0] * gain + shift).astype(BF)
-        kv[block_rows(r if ordered is None else table.tbl[r])] = (dot(low, w_kv) + kv_bias).astype(BF)
+        kv[pl.ds(pl.multiple_of(r * BLK, BLK), BLK)] = (dot(low, w_kv) + kv_bias).astype(BF)
         return carry
 
     lax.fori_loop(0, 2 * ctx, rows, 0)
@@ -408,14 +409,7 @@
     def own(i, carry):
         at = pl.ds(pl.multiple_of(i * BLK, BLK), BLK)
         low = (normed(tok[y, at].astype(F32))[0] * gain + shift).astype(BF)
-        if ordered is None:
-            h1[at] = low
-        else:
-            cot, tok_slots, cot_slots = ordered
-            at, stored = block_rows(jnp.where(i == 0, table.place[0], table.place[1])), at
-            h1[:, at] = jnp.transpose(low)
-            tok_slots[at] = tok[y, stored]
-            cot_slots[at] = cot[stored]
+        h1[at] = low
         q[at] = ((dot(low, w_q) + vec[2:3]).astype(BF).astype(F32) * HD ** (-0.5)).astype(BF)
         return carry
 
@@ -582,17 +576,13 @@
     return jax.ShapeDtypeStruct(dims, dtype)
 
 
-def attend_kernel(ctx, ordered, tbl, tok, wall, *rest):
+def attend_kernel(ctx, tbl, tok, wall, h1, q, kv, att, lse, vec, lse_acc):
     width = tok.shape[2]
     y = lax.axis_index("ctx")
-    table = Table(tbl, 2 * ctx, y, ordered)
-    extra = None
-    if ordered:
-        extra, rest = (rest[0], *rest[1:3]), rest[3:]
-    h1, q, kv, att, lse, vec, lse_acc = rest
+    table = Table(tbl, 2 * ctx, y)
     small = rows_of(wall, slice(None), slice(None), slice(0, 128)).astype(F32)
     vec[...] = jnp.transpose(small)[0:16]
-    project(ctx, table, tok, wall, h1, q, kv, vec, y, extra)
+    project(ctx, tok, wall, h1, q, kv, vec, y)
     lse_acc[...] = jnp.zeros_like(lse_acc)
 
     def pair(hp, carry):
@@ -604,19 +594,234 @@
         lse[slot] = jnp.transpose(lse_acc[slot])[0:16]
 
 
-def attend(tbl, tok_all, wall, ctx, cot=None):
+def attend(tbl, tok_all, wall, ctx):
     rows, width = tok_all.shape[1:]
-    ordered = cot is not None
-    slots = (shape(rows, width), shape(rows, width), shape(width, rows)) if ordered else (shape(rows, width),)
-    outs = slots + (shape(rows, width), shape(ctx * rows, 2 * width), shape(2, BLK, width),
-                    shape(2, 16, BLK, dtype=F32), shape(16, width, dtype=F32))
-    args = (tbl, tok_all, wall) + ((cot,) if ordered else ())
     return pl.pallas_call(
-        functools.partial(attend_kernel, ctx, ordered),
-        out_shape=outs, in_specs=[SM] + [VM] * (len(args) - 1), out_specs=(VM,) * len(outs),
+        functools.partial(attend_kernel, ctx),
+        out_shape=(shape(rows, width), shape(rows, width), shape(ctx * rows, 2 * width), shape(2, BLK, width),
+                   shape(2, 16, BLK, dtype=F32), shape(16, width, dtype=F32)),
+        in_specs=[SM, VM, VM], out_specs=(VM,) * 6,
         scratch_shapes=[pltpu.VMEM((2, BLK, LANES), F32)],
         compiler_params=params(62), name="attend",
-    )(*args)
+    )(tbl, tok_all, wall)
+
+
+def front_kernel(dp, ctx, tbl, tok, cot, *rest):
+    vectors, rest = rest[:8], rest[8:]
+    (b_up, w_qkv, w_out, w_up, w_down,
+     wall, tok_slots, cot_slots, h1, q, kv, att, lse, vec,
+     cat, small, toks, wq, lse_acc, loc, st, rt, sz, rz, sx, rx, sy, ry, sc, rc) = rest
+    at = Spot(dp, ctx)
+    lines = at.lines
+    r, full = cat.shape
+    width = tok.shape[1]
+    head = 128 + 3 * width
+    size = (full - head) // 6
+    ky = at.y
+    mate = {"dp": at.dp_at(at.z, at.x, 1 - at.c)}
+    across = {"dp": at.dp_at(at.z, 1 - at.x, at.c)}
+    pair_y = {"ctx": 1 - ky}
+    table = Table(tbl, 2 * ctx, at.y, True)
+    order = [0] + near_first(lines)
+
+    small[...] = jnp.zeros_like(small)
+    for i, ref in enumerate(vectors):
+        small[i:i + 1, 0:r] = ref[...].astype(F32).reshape(1, r)
+    small[8:12, 0:r] = b_up[...].astype(F32)
+    cat[:, 0:128] = jnp.transpose(small[...])[0:r].astype(BF)
+    cat[:, 128:head] = w_qkv[...]
+    cat[:, head:head + width] = w_out[...]
+    cat[:, head + width:head + 5 * width] = w_up[...]
+    for j in range(4):
+        cat[:, head + (5 + j) * width:head + (6 + j) * width] = w_down[j * r:(j + 1) * r]
+    at.barrier()
+
+    def cols(p):
+        if isinstance(p, int) and p >= 5:
+            place = 2 * (p - 4) + 1 - ky
+        else:
+            n = p - 1
+            place = (1 - n % 2) * (2 + 2 * (n // 2) + ky) + (n % 2) * (n // 2)
+        return pl.ds(pl.multiple_of(head + place * size, 128), size)
+
+    def is_head(p):
+        return isinstance(p, int) and p == 0
+
+    def own_block(p):
+        return cat.at[:, pl.ds(0, head)] if is_head(p) else cat.at[:, cols(p)]
+
+    def block(p, z, x, c):
+        return wq.at[at.dp_at(z, x, c)] if is_head(p) else wall.at[at.dp_at(z, x, c), :, cols(p)]
+
+    def to_z(p, k):
+        return remote(own_block(p), block(p, at.z, at.x, at.c), sz.at[p, k], rz.at[p, at.z],
+                      {"dp": at.dp_at(at.z_at(k), at.x, at.c)})
+
+    def to_x(p, k):
+        z = at.z_at(k)
+        src = own_block(p) if k == 0 else block(p, z, at.x, at.c)
+        return remote(src, block(p, z, at.x, at.c), sx.at[p, k], rx.at[p, z], across)
+
+    def to_c(p, k, kx):
+        z, x = at.z_at(k), (at.x + kx) % 2
+        src = own_block(p) if k == 0 and kx == 0 else block(p, z, x, at.c)
+        return remote(src, block(p, z, x, at.c), sc.at[p, k, kx], rc.at[p, z, x], mate)
+
+    def to_y(p, k, kx):
+        z, x = at.z_at(k), (at.x + kx) % 2
+        n = (p - 1) // 2
+        here = block(p, z, x, at.c)
+        return remote(here, here, sy.at[n, k, kx], ry.at[n, z, x], pair_y)
+
+    def got(p, z, x, c, sem):
+        here = block(p, z, x, c)
+        remote(here, here, st, sem, across).wait_recv()
+
+    def stage_z(p, shared):
+        for k in order:
+            if k:
+                got(p, at.z_at(k), at.x, at.c, rz.at[p, at.z_at(k)])
+                to_x(p, k).start()
+                if shared is not None:
+                    pl.when(shared)(lambda: to_y(p, k, 0).start())
+                to_c(p, k, 0).start()
+
+    def stage_x(p, shared):
+        for k in order:
+            got(p, at.z_at(k), 1 - at.x, at.c, rx.at[p, at.z_at(k)])
+            if shared is not None:
+                pl.when(shared)(lambda: to_y(p, k, 1).start())
+            to_c(p, k, 1).start()
+
+    def stage_y(n):
+        p = 5 + n
+        for kx in range(2):
+            for k in order:
+                if k or kx:
+                    z, x = at.z_at(k), (at.x + kx) % 2
+                    got(p, z, x, at.c, ry.at[n, z, x])
+                    to_c(p, k, kx).start()
+
+    def stage_c(p):
+        for kx in range(2):
+            for k in order:
+                z, x = at.z_at(k), (at.x + kx) % 2
+                got(p, z, x, 1 - at.c, rc.at[p, z, x])
+
+    tok_mate = remote(tok, toks.at[at.y], st, rt, pair_y)
+    tok_own = pltpu.make_async_copy(tok, toks.at[at.y], loc.at[0])
+    wall_own = pltpu.make_async_copy(cat.at[:, pl.ds(head, full - head)],
+                                     wall.at[at.me, :, pl.ds(head, full - head)], loc.at[1])
+    head_own = pltpu.make_async_copy(cat.at[:, pl.ds(0, head)], wq.at[at.me], loc.at[2])
+    to_x(0, 0).start()
+    for k in near_first(lines):
+        to_z(0, k).start()
+    to_c(0, 0, 0).start()
+    tok_mate.start()
+    for copy in (tok_own, head_own, wall_own):
+        copy.start()
+    for p in range(1, 5):
+        for k in near_first(lines):
+            to_z(p, k).start()
+        to_x(p, 0).start()
+    for p in range(1, 7):
+        to_c(p, 0, 0).start()
+    stage_z(0, None)
+    stage_x(0, None)
+    stage_c(0)
+    head_own.wait()
+    head_all = pltpu.make_async_copy(wq, wall.at[:, :, pl.ds(0, head)], loc.at[2])
+    head_all.start()
+    tok_own.wait()
+    tok_mate.wait_recv()
+
+    columns = jnp.transpose(rows_of(wq, slice(None), slice(None), slice(0, 128)).astype(F32))
+    vec[...] = columns[0:16]
+    gain, shift = vec[0:1], vec[1:2]
+    kv_bias = jnp.concatenate([jnp.zeros((1, width), F32), vec[3:4]], axis=1)
+
+    def stored(i):
+        return toks[i // 2, block_rows(i % 2)].astype(F32)
+
+    for j in range(2 * ctx):
+        here = stored(0)
+        for i in range(1, 2 * ctx):
+            here = jnp.where(tbl[i] == j, stored(i), here)
+        low = (normed(here)[0] * gain + shift).astype(BF)
+        kv[block_rows(j)] = (dot(low, rows_of(wq, slice(None), slice(None), slice(128 + width, head)))
+                             + kv_bias).astype(BF)
+    for i in range(2):
+        def chosen(ref):
+            a, b = ref[block_rows(i)].astype(F32), ref[block_rows(1 - i)].astype(F32)
+            return jnp.where(table.turned, b, a)
+
+        here = chosen(tok)
+        low = (normed(here)[0] * gain + shift).astype(BF)
+        h1[:, block_rows(i)] = jnp.transpose(low)
+        w_q = rows_of(wq, slice(None), slice(None), slice(128, 128 + width))
+        q[block_rows(i)] = ((dot(low, w_q) + vec[2:3]).astype(BF).astype(F32) * HD ** (-0.5)).astype(BF)
+        tok_slots[block_rows(i)] = here.astype(BF)
+        cot_slots[block_rows(i)] = chosen(cot).astype(BF)
+    lse_acc[...] = jnp.zeros_like(lse_acc)
+
+    def heads(hp, carry):
+        attend_pair(hp, table, q, kv, att, lse_acc, width)
+        return carry
+
+    def stages(t, carry):
+        @pl.when(t < 4)
+        def _():
+            stage_z(t + 1, t % 2 == 0)
+
+        @pl.when(t >= 1)
+        def _():
+            stage_x(t, t % 2 == 1)
+
+        lax.fori_loop(jnp.minimum(2 * t, PAIRS), jnp.minimum(2 * t + 2, PAIRS), heads, 0)
+        return carry
+
+    lax.fori_loop(0, 5, stages, 0)
+    for slot in range(2):
+        lse[slot] = jnp.transpose(lse_acc[slot])[0:16]
+    stage_y(0)
+    stage_y(1)
+    for p in range(1, 7):
+        stage_c(p)
+    for p in range(5):
+        for k in order:
+            to_x(p, k).wait_send()
+            if k:
+                to_z(p, k).wait_send()
+    for p in range(7):
+        for kx in range(2):
+            for k in order:
+                to_c(p, k, kx).wait_send()
+                if p in (1, 3) and (k or kx):
+                    to_y(p, k, kx).wait_send()
+    tok_mate.wait_send()
+    wall_own.wait()
+    head_all.wait()
+
+
+def front(tbl, tok, cot, vectors, b_up, weights, dp, ctx):
+    rows, width = tok.shape
+    r = weights[0].shape[0]
+    head = 128 + 3 * width
+    full = head + 9 * width
+    lines = dp // 4
+    V = pltpu.VMEM
+    return pl.pallas_call(
+        functools.partial(front_kernel, dp, ctx),
+        out_shape=(shape(dp, r, full), shape(rows, width), shape(rows, width), shape(width, rows), shape(rows, width),
+                   shape(ctx * rows, 2 * width), shape(2, BLK, width), shape(2, 16, BLK, dtype=F32),
+                   shape(16, width, dtype=F32)),
+        in_specs=[SM] + [VM] * (2 + len(vectors) + 1 + len(weights)), out_specs=(ANY,) + (VM,) * 8,
+        scratch_shapes=[V((r, full), BF), V((128, 128), F32), V((ctx, rows, width), BF), V((dp, r, head), BF),
+                        V((2, BLK, LANES), F32), DMA((3,)), DMA, DMA,
+                        DMA((5, lines)), DMA((5, lines)), DMA((5, lines)), DMA((5, lines)),
+                        DMA((2, lines, 2)), DMA((2, lines, 2)), DMA((7, lines, 2)), DMA((7, lines, 2))],
+        compiler_params=params(62, collective_id=0, has_side_effects=True), name="front",
+    )(tbl, tok, cot, *vectors, b_up, *weights)
 
 
 def feed_kernel(ctx, nd, off_up, off_down, tbl, tok, att, wall, cot, vec, bup, *rest):
@@ -1078,6 +1283,43 @@
     )(tbl, tok, att, cot, q, kv, h1t, lse, vec, bup, wall)
 
 
+def finish_kernel(count, *refs):
+    ins, small, outs = refs[:count], refs[count], refs[count + 1:2 * count + 1]
+    vectors, rest = refs[2 * count + 1:2 * count + 10], refs[2 * count + 10:]
+    held, fetched, given = rest[:count], rest[count], rest[count + 1]
+
+    def fetch(i):
+        return pltpu.make_async_copy(ins[i], held[i], fetched.at[i])
+
+    def give(i):
+        return pltpu.make_async_copy(held[i], outs[i], given.at[i])
+
+    for i in range(count):
+        fetch(i).start()
+    r = small.shape[0]
+    total = jnp.transpose(jnp.concatenate([small[...], jnp.zeros((128 - r, 128), F32)], axis=0))
+    for i in range(8):
+        vectors[i][...] = total[i:i + 1, 0:r].reshape(r)
+    vectors[8][...] = total[8:12, 0:r]
+    for i in range(count):
+        fetch(i).wait()
+        give(i).start()
+    for i in range(count):
+        give(i).wait()
+
+
+def finish(results, small):
+    count, r = len(results), small.shape[0]
+    outs = tuple(jax.ShapeDtypeStruct(a.shape, a.dtype) for a in results)
+    return pl.pallas_call(
+        functools.partial(finish_kernel, count),
+        out_shape=outs + (shape(r, dtype=F32),) * 8 + (shape(4, r, dtype=F32),),
+        in_specs=[HBM] * count + [VM], out_specs=(HBM,) * count + (VM,) * 9,
+        scratch_shapes=[pltpu.VMEM(a.shape, a.dtype) for a in results] + [DMA((count,)), DMA((count,))],
+        compiler_params=pltpu.CompilerParams(vmem_limit_bytes=67043328), name="finish",
+    )(*results, small)
+
+
 def shards(tokens, block_table, ln1_gain, ln1_bias, w_qkv, bias_query, bias_value, w_out, bias_out,
            ln2_gain, ln2_bias, w_up, bias_up, w_down, bias_down, cotangent):
     dp, ctx = lax.axis_size("dp"), lax.axis_size("ctx")
@@ -1087,19 +1329,21 @@
     third = (width + 2 * hidden) // 3
     off_up = head + width
     off_down = off_up + hidden
-    small = jnp.concatenate([jnp.stack([ln1_gain, ln1_bias, bias_query, bias_value, bias_out, ln2_gain, ln2_bias,
-                                        bias_down]), bias_up.reshape(4, r), jnp.zeros((116, r), BF)]).T
+    vectors = [ln1_gain, ln1_bias, bias_query, bias_value, bias_out, ln2_gain, ln2_bias, bias_down]
+    if ctx == 2 and dp == 16:
+        wall, tok, cot, h1, q, kv, att, lse, vec = front(
+            block_table, tokens[0], cotangent[0], vectors, bias_up.reshape(4, r), (w_qkv, w_out, w_up, w_down), dp, ctx)
+        bup = vec[8:12].reshape(4, dp, r).transpose(1, 0, 2).reshape(1, hidden)
+        out, gtok, g_small, g_qkv, g_out, g_up, g_down = backward(
+            block_table, tok, att, cot, q, kv, h1, lse, vec, bup, wall, ctx)
+        out, gtok, g_qkv, g_out, g_up, g_down, *rows = finish((out, gtok, g_qkv, g_out, g_up, g_down), g_small)
+        return (out[None], gtok[None], rows[0], rows[1], g_qkv, rows[2], rows[3], g_out, rows[4], rows[5], rows[6],
+                g_up, rows[8].reshape(4 * r), g_down, rows[7])
+    small = jnp.concatenate([jnp.stack(vectors), bias_up.reshape(4, r), jnp.zeros((116, r), BF)]).T
     cat = jnp.concatenate([small, w_qkv, w_out, w_up] + [w_down[j * r:(j + 1) * r] for j in range(4)], axis=1)
     tok_all, wall = gather(tokens[0], cat, dp, ctx, head, third)
-    fused = ctx == 2 and dp == 16
-    *slots, h1, q, kv, att, lse, vec = attend(block_table, tok_all, wall, ctx, cotangent[0] if fused else None)
+    h1, q, kv, att, lse, vec = attend(block_table, tok_all, wall, ctx)
     bup = vec[8:12].reshape(4, dp, r).transpose(1, 0, 2).reshape(1, hidden)
-    if fused:
-        out, gtok, g_small, g_qkv, g_out, g_up, g_down = backward(
-            block_table, slots[0], att, slots[1], q, kv, h1, lse, vec, bup, wall, ctx)
-        rows = g_small.T
-        return (out[None], gtok[None], rows[0], rows[1], g_qkv, rows[2], rows[3], g_out, rows[4], rows[5], rows[6],
-                g_up, rows[8:12].reshape(4 * r), g_down, rows[7])
     out, gt, da, dx1, delta, gvec, gup = feed_call(block_table, tokens[0], att, wall, cotangent[0], vec, bup,
                                                    ctx, off_up, off_down, 3 * third)
     dq, dkv = attend_back(block_table, q, kv, da, lse, delta, ctx)

time: 261 us -> 219 us (0.84)
  local copies, waits for them, and re-layouts: 33 us -> 4.16 us
  Pallas kernels: 226 us -> 214 us
    unnamed x27 -> x0, local copies, waits for them, and re-layouts: 20.1 us -> none
    pallas_call x2, Pallas kernels: 109 us -> 97.6 us  [the longest x1 93.3 us: front(): pl.pallas_call(functools.partial(front_kernel, dp, ctx), out_shape=(shape...]
    another operation x8 -> x0, local copies, waits for them, and re-layouts: 6.05 us -> none  [shards(): jnp.stack([ln1_gain, ln1_bias, bias_query, bias_value, bias_out, ln2_gain...]
    slice x3 -> x0, local copies, waits for them, and re-layouts: 2.77 us -> none  [the longest x1 1.88 us: shards(): rows[7]]
where the time goes in v3:
time: 219 us; the launch traced here: 218 us
  Pallas kernels  214 us (98%)
  local copies, waits for them, and re-layouts  4.16 us (2%)
    pallas_call x1, Pallas kernels, backward(): pl.pallas_call(functools.partial(backward_kernel, dp, ctx), out_shape=(sh...  116 us
    pallas_call x1, Pallas kernels, front(): pl.pallas_call(functools.partial(front_kernel, dp, ctx), out_shape=(shape...  93.3 us

profile of v3, /device:TPU:0, one launch (start us, length us, event | category | flops | bytes accessed | tf_op | source)
XLA Modules:
  0.0 218.4 jit_solution(15219462736298592745)
XLA Ops:
  0.6 1.3 reshape.42.rest_8_
  1.9 93.3 %front.1 = (bf16[16,48,9344]{2,1,0:T(8,128)(2,1)}, bf16[512,768]{1,0:T(8,128)(2,1)}, bf16[512,768]{1,0:T(8,128)(2,1)}, bf16[768,512]{1,0:T(8,128)(2,1)}, bf16[51...) custom-call(s32[4]{0:T(128)} %tbl.3, ...), custom_call_target="tpu_custom_call" | custom-call | tf_op jit(solution)/shard_map/front/pallas_call | solution.py:813
  95.3 0.7 slice.3
  96.0 0.1 reshape.43
  96.1 0.7 reshape.44.bup
  96.8 115.9 %backward.1 = (bf16[512,768]{1,0:T(8,128)(2,1)}, bf16[512,768]{1,0:T(8,128)(2,1)}, f32[48,128]{1,0:T(8,128)}, f32[48,2304]{1,0:T(8,128)}, f32[48,768]{1,0:T(8,12...) custom-call(s32[4]{0:T(128)} %tbl.3, bf16[512,768]{1,0:T(8,128)(2,1)} %get-tuple-element.46.tok, ...), custom_call_target="tpu_custom_call" | custom-call | tf_op jit(solution)/shard_map/backward/pallas_call | solution.py:1265
  212.7 4.3 %finish.1 = (bf16[512,768]{1,0:T(8,128)(2,1)}, bf16[512,768]{1,0:T(8,128)(2,1)}, f32[48,2304]{1,0:T(8,128)}, f32[48,768]{1,0:T(8,128)}, f32[48,3072]{1,0:T(8,128...) custom-call(bf16[512,768]{1,0:T(8,128)(2,1)} %get-tuple-element.55.r, ...), custom_call_target="tpu_custom_call" | custom-call | tf_op jit(solution)/shard_map/finish/pallas_call | solution.py:1314
  217.1 1.3 reshape.45
  (1 shorter events, 0.0 us)

commit v4 on v3

--- a/solution.py
+++ b/solution.py
@@ -609,8 +609,8 @@
 def front_kernel(dp, ctx, tbl, tok, cot, *rest):
     vectors, rest = rest[:8], rest[8:]
     (b_up, w_qkv, w_out, w_up, w_down,
-     wall, tok_slots, cot_slots, h1, q, kv, att, lse, vec,
-     cat, small, toks, wq, lse_acc, loc, st, rt, sz, rz, sx, rx, sy, ry, sc, rc) = rest
+     wall, tok_slots, cot_slots, h1, q, kv, att, lse, vec, bup,
+     cat, small, tall, toks, wq, lse_acc, loc, st, rt, sz, rz, sx, rx, sy, ry, sc, rc) = rest
     at = Spot(dp, ctx)
     lines = at.lines
     r, full = cat.shape
@@ -627,7 +627,9 @@
     small[...] = jnp.zeros_like(small)
     for i, ref in enumerate(vectors):
         small[i:i + 1, 0:r] = ref[...].astype(F32).reshape(1, r)
-    small[8:12, 0:r] = b_up[...].astype(F32)
+    ups = b_up[...].astype(F32).reshape(1, 4 * r)
+    for j in range(4):
+        small[8 + j:9 + j, 0:r] = ups[:, j * r:(j + 1) * r]
     cat[:, 0:128] = jnp.transpose(small[...])[0:r].astype(BF)
     cat[:, 128:head] = w_qkv[...]
     cat[:, head:head + width] = w_out[...]
@@ -737,6 +739,11 @@
 
     columns = jnp.transpose(rows_of(wq, slice(None), slice(None), slice(0, 128)).astype(F32))
     vec[...] = columns[0:16]
+    for d in range(dp):
+        for j in range(4):
+            tall[(4 * d + j) * r:(4 * d + j + 1) * r] = jnp.broadcast_to(
+                wq[d, :, 0:128].astype(F32)[:, 8 + j:9 + j], (r, 128))
+    bup[...] = jnp.transpose(tall[...])[0:1]
     gain, shift = vec[0:1], vec[1:2]
     kv_bias = jnp.concatenate([jnp.zeros((1, width), F32), vec[3:4]], axis=1)
 
@@ -814,9 +821,9 @@
         functools.partial(front_kernel, dp, ctx),
         out_shape=(shape(dp, r, full), shape(rows, width), shape(rows, width), shape(width, rows), shape(rows, width),
                    shape(ctx * rows, 2 * width), shape(2, BLK, width), shape(2, 16, BLK, dtype=F32),
-                   shape(16, width, dtype=F32)),
-        in_specs=[SM] + [VM] * (2 + len(vectors) + 1 + len(weights)), out_specs=(ANY,) + (VM,) * 8,
-        scratch_shapes=[V((r, full), BF), V((128, 128), F32), V((ctx, rows, width), BF), V((dp, r, head), BF),
+                   shape(16, width, dtype=F32), shape(1, 4 * width, dtype=F32)),
+        in_specs=[SM] + [VM] * (2 + len(vectors) + 1 + len(weights)), out_specs=(ANY,) + (VM,) * 9,
+        scratch_shapes=[V((r, full), BF), V((128, 128), F32), V((4 * width, 128), F32), V((ctx, rows, width), BF), V((dp, r, head), BF),
                         V((2, BLK, LANES), F32), DMA((3,)), DMA, DMA,
                         DMA((5, lines)), DMA((5, lines)), DMA((5, lines)), DMA((5, lines)),
                         DMA((2, lines, 2)), DMA((2, lines, 2)), DMA((7, lines, 2)), DMA((7, lines, 2))],
@@ -1300,7 +1307,7 @@
     total = jnp.transpose(jnp.concatenate([small[...], jnp.zeros((128 - r, 128), F32)], axis=0))
     for i in range(8):
         vectors[i][...] = total[i:i + 1, 0:r].reshape(r)
-    vectors[8][...] = total[8:12, 0:r]
+    vectors[8][...] = jnp.concatenate([total[8 + j:9 + j, 0:r] for j in range(4)], axis=1).reshape(4 * r)
     for i in range(count):
         fetch(i).wait()
         give(i).start()
@@ -1313,7 +1320,7 @@
     outs = tuple(jax.ShapeDtypeStruct(a.shape, a.dtype) for a in results)
     return pl.pallas_call(
         functools.partial(finish_kernel, count),
-        out_shape=outs + (shape(r, dtype=F32),) * 8 + (shape(4, r, dtype=F32),),
+        out_shape=outs + (shape(r, dtype=F32),) * 8 + (shape(4 * r, dtype=F32),),
         in_specs=[HBM] * count + [VM], out_specs=(HBM,) * count + (VM,) * 9,
         scratch_shapes=[pltpu.VMEM(a.shape, a.dtype) for a in results] + [DMA((count,)), DMA((count,))],
         compiler_params=pltpu.CompilerParams(vmem_limit_bytes=67043328), name="finish",
@@ -1331,14 +1338,13 @@
     off_down = off_up + hidden
     vectors = [ln1_gain, ln1_bias, bias_query, bias_value, bias_out, ln2_gain, ln2_bias, bias_down]
     if ctx == 2 and dp == 16:
-        wall, tok, cot, h1, q, kv, att, lse, vec = front(
-            block_table, tokens[0], cotangent[0], vectors, bias_up.reshape(4, r), (w_qkv, w_out, w_up, w_down), dp, ctx)
-        bup = vec[8:12].reshape(4, dp, r).transpose(1, 0, 2).reshape(1, hidden)
+        wall, tok, cot, h1, q, kv, att, lse, vec, bup = front(
+            block_table, tokens[0], cotangent[0], vectors, bias_up, (w_qkv, w_out, w_up, w_down), dp, ctx)
         out, gtok, g_small, g_qkv, g_out, g_up, g_down = backward(
             block_table, tok, att, cot, q, kv, h1, lse, vec, bup, wall, ctx)
         out, gtok, g_qkv, g_out, g_up, g_down, *rows = finish((out, gtok, g_qkv, g_out, g_up, g_down), g_small)
         return (out[None], gtok[None], rows[0], rows[1], g_qkv, rows[2], rows[3], g_out, rows[4], rows[5], rows[6],
-                g_up, rows[8].reshape(4 * r), g_down, rows[7])
+                g_up, rows[8], g_down, rows[7])
     small = jnp.concatenate([jnp.stack(vectors), bias_up.reshape(4, r), jnp.zeros((116, r), BF)]).T
     cat = jnp.concatenate([small, w_qkv, w_out, w_up] + [w_down[j * r:(j + 1) * r] for j in range(4)], axis=1)
     tok_all, wall = gather(tokens[0], cat, dp, ctx, head, third)

time: 219 us -> 215 us (0.982)
  local copies, waits for them, and re-layouts: 4.16 us -> 0 us
    reshape x5 -> x0, local copies, waits for them, and re-layouts: 3.42 us -> none  [the longest x1 1.31 us: shards(): rows[8].reshape(4 * r)]
where the time goes in v4:
time: 215 us; the launch traced here: 214 us
  Pallas kernels  213 us (99%)
    pallas_call x1, Pallas kernels, backward(): pl.pallas_call(functools.partial(backward_kernel, dp, ctx), out_shape=(sh...  116 us
    pallas_call x1, Pallas kernels, front(): pl.pallas_call(functools.partial(front_kernel, dp, ctx), out_shape=(shape...  93.1 us
    pallas_call x1, Pallas kernels, finish(): pl.pallas_call(functools.partial(finish_kernel, count), out_shape=outs +...  4.3 us

profile of v4, /device:TPU:0, one launch (start us, length us, event | category | flops | bytes accessed | tf_op | source)
XLA Modules:
  0.0 214.3 jit_solution(12835785059916146780)
XLA Ops:
  0.7 93.1 %front.1 = (bf16[16,48,9344]{2,1,0:T(8,128)(2,1)}, bf16[512,768]{1,0:T(8,128)(2,1)}, bf16[512,768]{1,0:T(8,128)(2,1)}, bf16[768,512]{1,0:T(8,128)(2,1)}, bf16[51...) custom-call(s32[4]{0:T(128)} %tbl.3, ...), custom_call_target="tpu_custom_call" | custom-call | tf_op jit(solution)/shard_map/front/pallas_call | solution.py:820
  93.7 116.1 %backward.1 = (bf16[512,768]{1,0:T(8,128)(2,1)}, bf16[512,768]{1,0:T(8,128)(2,1)}, f32[48,128]{1,0:T(8,128)}, f32[48,2304]{1,0:T(8,128)}, f32[48,768]{1,0:T(8,12...) custom-call(s32[4]{0:T(128)} %tbl.3, bf16[512,768]{1,0:T(8,128)(2,1)} %get-tuple-element.47.tok, ...), custom_call_target="tpu_custom_call" | custom-call | tf_op jit(solution)/shard_map/backward/pallas_call | solution.py:1272
  209.8 4.3 %finish.1 = (bf16[512,768]{1,0:T(8,128)(2,1)}, bf16[512,768]{1,0:T(8,128)(2,1)}, f32[48,2304]{1,0:T(8,128)}, f32[48,768]{1,0:T(8,128)}, f32[48,3072]{1,0:T(8,128...) custom-call(bf16[512,768]{1,0:T(8,128)(2,1)} %get-tuple-element.57.r, ...), custom_call_target="tpu_custom_call" | custom-call | tf_op jit(solution)/shard_map/finish/pallas_call | solution.py:1321

commit v5 on v4

--- a/solution.py
+++ b/solution.py
@@ -643,7 +643,7 @@
             place = 2 * (p - 4) + 1 - ky
         else:
             n = p - 1
-            place = (1 - n % 2) * (2 + 2 * (n // 2) + ky) + (n % 2) * (n // 2)
+            place = (1 - n // 2) * (2 + 2 * n + ky) + (n // 2) * (n - 2)
         return pl.ds(pl.multiple_of(head + place * size, 128), size)
 
     def is_head(p):
@@ -671,7 +671,7 @@
 
     def to_y(p, k, kx):
         z, x = at.z_at(k), (at.x + kx) % 2
-        n = (p - 1) // 2
+        n = p - 1
         here = block(p, z, x, at.c)
         return remote(here, here, sy.at[n, k, kx], ry.at[n, z, x], pair_y)
 
@@ -710,20 +710,22 @@
                 z, x = at.z_at(k), (at.x + kx) % 2
                 got(p, z, x, 1 - at.c, rc.at[p, z, x])
 
+    low_end, high_end = (at.z == 0).astype(jnp.int32), (at.z == 3).astype(jnp.int32)
+    nearest = [1 + 2 * high_end, 3 - low_end - high_end, 2 + low_end - high_end]
     tok_mate = remote(tok, toks.at[at.y], st, rt, pair_y)
     tok_own = pltpu.make_async_copy(tok, toks.at[at.y], loc.at[0])
     wall_own = pltpu.make_async_copy(cat.at[:, pl.ds(head, full - head)],
                                      wall.at[at.me, :, pl.ds(head, full - head)], loc.at[1])
     head_own = pltpu.make_async_copy(cat.at[:, pl.ds(0, head)], wq.at[at.me], loc.at[2])
     to_x(0, 0).start()
-    for k in near_first(lines):
+    for k in nearest:
         to_z(0, k).start()
     to_c(0, 0, 0).start()
     tok_mate.start()
     for copy in (tok_own, head_own, wall_own):
         copy.start()
     for p in range(1, 5):
-        for k in near_first(lines):
+        for k in nearest:
             to_z(p, k).start()
         to_x(p, 0).start()
     for p in range(1, 7):
@@ -778,11 +780,11 @@
     def stages(t, carry):
         @pl.when(t < 4)
         def _():
-            stage_z(t + 1, t % 2 == 0)
+            stage_z(t + 1, t < 2)
 
         @pl.when(t >= 1)
         def _():
-            stage_x(t, t % 2 == 1)
+            stage_x(t, t < 3)
 
         lax.fori_loop(jnp.minimum(2 * t, PAIRS), jnp.minimum(2 * t + 2, PAIRS), heads, 0)
         return carry
@@ -803,7 +805,7 @@
         for kx in range(2):
             for k in order:
                 to_c(p, k, kx).wait_send()
-                if p in (1, 3) and (k or kx):
+                if p in (1, 2) and (k or kx):
                     to_y(p, k, kx).wait_send()
     tok_mate.wait_send()
     wall_own.wait()

time: 215 us -> 213 us (level)
  no operation moved by 1% of the time
where the time goes in v5:
time: 213 us
  Pallas kernels  212 us (100%)
    pallas_call x1, Pallas kernels, backward(): pl.pallas_call(functools.partial(backward_kernel, dp, ctx), out_shape=(sh...  116 us
    pallas_call x1, Pallas kernels, front(): pl.pallas_call(functools.partial(front_kernel, dp, ctx), out_shape=(shape...  91.8 us
    pallas_call x1, Pallas kernels, finish(): pl.pallas_call(functools.partial(finish_kernel, count), out_shape=outs +...  4.3 us

profile of v5, /device:TPU:0, one launch (start us, length us, event | category | flops | bytes accessed | tf_op | source)
XLA Modules:
  0.0 212.8 jit_solution(1449789159265220835)
XLA Ops:
  0.7 91.8 %front.1 = (bf16[16,48,9344]{2,1,0:T(8,128)(2,1)}, bf16[512,768]{1,0:T(8,128)(2,1)}, bf16[512,768]{1,0:T(8,128)(2,1)}, bf16[768,512]{1,0:T(8,128)(2,1)}, bf16[51...) custom-call(s32[4]{0:T(128)} %tbl.3, ...), custom_call_target="tpu_custom_call" | custom-call | tf_op jit(solution)/shard_map/front/pallas_call | solution.py:822
  92.4 115.9 %backward.1 = (bf16[512,768]{1,0:T(8,128)(2,1)}, bf16[512,768]{1,0:T(8,128)(2,1)}, f32[48,128]{1,0:T(8,128)}, f32[48,2304]{1,0:T(8,128)}, f32[48,768]{1,0:T(8,12...) custom-call(s32[4]{0:T(128)} %tbl.3, bf16[512,768]{1,0:T(8,128)(2,1)} %get-tuple-element.47.tok, ...), custom_call_target="tpu_custom_call" | custom-call | tf_op jit(solution)/shard_map/backward/pallas_call | solution.py:1274
  208.4 4.3 %finish.1 = (bf16[512,768]{1,0:T(8,128)(2,1)}, bf16[512,768]{1,0:T(8,128)(2,1)}, f32[48,2304]{1,0:T(8,128)}, f32[48,768]{1,0:T(8,128)}, f32[48,3072]{1,0:T(8,128...) custom-call(bf16[512,768]{1,0:T(8,128)(2,1)} %get-tuple-element.57.r, ...), custom_call_target="tpu_custom_call" | custom-call | tf_op jit(solution)/shard_map/finish/pallas_call | solution.py:1323
